TPU v7x, 256 devices: a whole 4x4x8 slice. The times are simulated.
256 devices in a mesh: row: 32 (over y, z), col: 8 (over x, core).
Axes of the slice: x: 4, y: 4, z: 8, core: 2. Of those that a mesh axis runs over, the one named last changes fastest.
Arguments:
- grams: bfloat16 [4, 3584, 3584], P(None, 'row', 'col'), as said below
- weights: bfloat16 [4, 3584, 7168], P(None, 'row', 'col'), may hold values from -6 to 6
Outputs:
- merged: float32 [3584, 7168], P('row', 'col')
- residual: float32 [3584, 7168], P('row', 'col')
Inputs may be any that keep to these rules, and one draw needn't show every extreme that they name: `grams`: each of the 4 matrices is symmetric and positive definite.
All inputs are finite; a program needn't handle non-finite values.
Results may differ from a plain program's by a relative error of at most 0.012.
The roundings to bfloat16 on the way count: a program that leaves them out, or rounds other values in their place, can miss the bound.
Values may be sent and summed in bfloat16 or wider, within the bound.
No kernel may reach another device: no remote copies, remote signals or barrier semaphores. Data moves between devices by JAX's collectives and lax.ppermute only.
A program may use at most 256 MiB of HBM per device.

v0:
```python
import jax
import jax.numpy as jnp
from jax import lax
from jax.sharding import Mesh
from jax.sharding import PartitionSpec as P

ITERS = 2
ROW = ("row_0", "row_1")


def sum_by_axis(so_far, axes):
    for axis in axes:
        so_far = lax.psum_scatter(so_far, axis, scatter_dimension=0, tiled=True)
    return so_far


def sent_to_all(x, axis):
    copies = jnp.broadcast_to(x, (lax.axis_size(axis), *x.shape))
    return lax.all_to_all(copies, axis, split_axis=0, concat_axis=0, tiled=True)


def of_everyone(x, axis):
    return sent_to_all(x, axis).sum(axis=0)


def together(arrays, axis):
    ravelled, at, done = (jnp.concatenate([a.reshape(-1) for a in arrays]), 0, [])
    so_far = of_everyone(ravelled, axis)
    for a in arrays:
        done.append(so_far[at : at + a.size].reshape(a.shape))
        at += a.size
    return tuple(done)


def shards(grams, weights):
    slab_rows = grams.shape[1]
    col_count = weights.shape[2]
    first_row = lax.axis_index(ROW) * slab_rows
    high = lax.Precision.HIGHEST
    gram_slabs = lax.all_gather(grams, "col", axis=2, tiled=True)
    gram_total = jnp.sum(gram_slabs, axis=0, dtype=jnp.float32)
    square_block = lax.dynamic_slice_in_dim(gram_slabs, first_row, slab_rows, gram_slabs.ndim - 1)
    diag_total = jnp.einsum(
        "mr,mrc->rc",
        jnp.diagonal(square_block, axis1=-2, axis2=-1).astype(jnp.float32),
        weights.astype(jnp.float32),
    )
    product = sum_by_axis(
        jnp.einsum("mrk,mrc->kc", gram_slabs, weights, preferred_element_type=jnp.float32), ROW
    )
    right_side = 0.9 * product + 0.1 * diag_total
    total_diag = jnp.diagonal(lax.dynamic_slice_in_dim(gram_total, first_row, slab_rows, 1))
    merged = jnp.zeros((slab_rows, col_count), jnp.float32)
    residual = right_side
    direction = right_side
    for iteration in range(ITERS):
        rounded = direction.astype(jnp.bfloat16)
        shard_piece = lax.all_gather(rounded, ROW, axis=0, tiled=True)
        add_columns = lax.slice_in_dim(gram_total, 0, shard_piece.shape[0], axis=1)
        mapped = jnp.zeros((slab_rows, col_count), jnp.float32) + jnp.dot(
            add_columns, shard_piece.astype(jnp.float32), precision=high
        )
        mapped = 0.9 * mapped + 0.1 * total_diag[:, None] * rounded.astype(jnp.float32)
        curvature, cross_term, square, norm_now = together(
            (
                jnp.sum(direction * mapped, axis=0),
                jnp.sum(residual * mapped, axis=0),
                jnp.sum(mapped * mapped, axis=0),
                jnp.sum(residual * residual, axis=0),
            ),
            ROW,
        )
        step_length = norm_now / curvature
        merged = merged + step_length * direction
        residual = residual - step_length * mapped
        if iteration + 1 < ITERS:
            norm_next = (
                norm_now - 2.0 * step_length * cross_term + step_length * step_length * square
            )
            direction = residual + norm_next / norm_now * direction
    return (merged, residual)


def solution(mesh):
    torus = Mesh(mesh.devices.reshape(4, 8, mesh.shape["col"]), ("row_0", "row_1", "col"))
    in_specs = (P(None, ROW, "col"), P(None, ROW, "col"))
    out_specs = (P(ROW, "col"), P(ROW, "col"))
    return jax.shard_map(
        shards, mesh=torus, in_specs=in_specs, out_specs=out_specs, check_vma=False
    )
```

profile of v0, /device:TPU:32, one launch (start us, length us, event | category | flops | bytes accessed | tf_op | source)
XLA Modules:
  0.0 467.3 jit_solution(11836406161750740182)
XLA Ops:
  7.2 2.1 copy.14
  9.4 35.5 %all-gather.4.cloned.1.call-done = bf16[4,112,3584]{1,2,0:T(8,128)(2,1)} async-done(((bf16[4,112,448]{1,2,0:T(8,128)(2,1)}), bf16[4,112,3584]{1,2,0:T(8,128)(2,1)}) %all-gather.4.cloned.1.call-update) | async-done | bytes 3211280 | tf_op jit(solution)/shard_map/all_gather | solution.py:40
  44.9 8.9 %convolution_bitcast_fusion = f32[3584,896]{1,0:T(8,128)} fusion(bf16[4,112,3584]{1,2,0:T(8,128)(2,1)} %all-gather.4.cloned.1.call-done, bf16[4,112,896]{2,1,0:T(8,128)(2,1)S(1)} %copy-done), kind=kOutput, calls=%fused_computation.2 | convolution fusion | flops 2877292544 | bytes 16859136 | tf_op jit(solution)/shard_map/mrk,mrc->kc/dot_general | solution.py:49
  53.8 119.3 %reduce-scatter.3.cloned.1.call-done = f32[896,896]{1,0:T(8,128)} async-done(((f32[3584,896]{1,0:T(8,128)}), f32[896,896]{1,0:T(8,128)}) %reduce-scatter.3.cloned.1.call-update) | async-done | bytes 3211280 | tf_op jit(solution)/shard_map/reduce_scatter | solution.py:13
  173.2 0.9 constant_dynamic-slice_fusion.1
  174.1 3.2 copy.15
  177.3 2.9 gather_fusion
  180.2 0.6 fusion.2
  180.8 41.3 %reduce-scatter.5.cloned.1.call-done = f32[112,896]{1,0:T(8,128)} async-done(((f32[896,896]{1,0:T(8,128)}), f32[112,896]{1,0:T(8,128)}) %reduce-scatter.5.cloned.1.call-update) | async-done | bytes 401424 | tf_op jit(solution)/shard_map/reduce_scatter | solution.py:13
  222.1 1.8 fusion.10
  223.9 3.0 convert_reduce_fusion
  227.1 1.7 gather_fusion.1
  228.8 85.2 %all-gather.6.cloned.1.call-done = bf16[3584,896]{1,0:T(8,128)(2,1)} async-done(((bf16[112,896]{1,0:T(8,128)(2,1)}), bf16[3584,896]{1,0:T(8,128)(2,1)}) %all-gather.6.cloned.1.call-update) | async-done | bytes 6422544 | tf_op jit(solution)/shard_map/all_gather | solution.py:58
  314.0 7.0 %multiply_reduce_fusion.6 = (f32[896]{0:T(1024)S(1)}, f32[896]{0:T(1024)S(1)}, f32[896]{0:T(1024)S(1)}, f32[112,896]{1,0:T(8,128)}) fusion(f32[112,896]{1,0:T(8,128)S(1)} %get-tuple-element.14, bf16[112,896]{1,0:T(8,128)(2,1)S(1)} %copy-done.1, f32[112]{0:T(128)S(1)} %broadcast_multiply_fusion, f32[112,3584]{0,1:T(8,128)S(1)} %convert_reduce_fusion, ...), kind=kOutput, calls=%fused_computation.22 | convolution fusion | flops 4316939776 | bytes 9042880 | tf_op jit(solution)/shard_map/dot_general | solution.py:60
  320.9 0.2 broadcast_in_dim.12
  321.2 21.5 %all_to_all.12 = f32[32,1,3584]{2,1,0:T(1,128)S(1)} all-to-all(f32[32,1,3584]{2,1,0:T(1,128)S(1)} %broadcast_in_dim.12), channel_id=1, replica_groups=mesh['row_0'=4,'row_1'=8,'col'=8] {'row_0','row_1'}, dimensions={0} | all-to-all | bytes 917504 | tf_op jit(solution)/shard_map/all_to_all | solution.py:19
  342.7 0.3 reduce_sum.98
  343.0 1.7 fusion.5
  344.8 84.9 %all-gather.8.cloned.1.call-done = bf16[3584,896]{1,0:T(8,128)(2,1)} async-done(((bf16[112,896]{1,0:T(8,128)(2,1)}), bf16[3584,896]{1,0:T(8,128)(2,1)}) %all-gather.8.cloned.1.call-update) | async-done | bytes 6422544 | tf_op jit(solution)/shard_map/all_gather | solution.py:58
  429.7 7.0 %multiply_reduce_fusion.3 = (f32[896]{0:T(1024)S(1)}, f32[896]{0:T(1024)S(1)}, f32[896]{0:T(1024)S(1)}, f32[896]{0:T(1024)S(1)}, f32[112,896]{1,0:T(8,128)}) fusion(f32[112,896]{1,0:T(8,128)S(1)} %get-tuple-element.10, f32[112,896]{1,0:T(8,128)S(1)} %get-tuple-element.14, f32[896]{0:T(1024)S(1)} %get-tuple-element.11, ...), kind=kOutput, calls=%fused_computation.17 | convolution fusion | flops 4317340160 | bytes 9451456 | tf_op jit(solution)/shard_map/dot_general | solution.py:60
  436.7 0.2 broadcast_in_dim.13
  437.0 21.5 %all_to_all.13 = f32[32,1,3584]{2,1,0:T(1,128)S(1)} all-to-all(f32[32,1,3584]{2,1,0:T(1,128)S(1)} %broadcast_in_dim.13), channel_id=1, replica_groups=mesh['row_0'=4,'row_1'=8,'col'=8] {'row_0','row_1'}, dimensions={0} | all-to-all | bytes 917504 | tf_op jit(solution)/shard_map/all_to_all | solution.py:19
  458.5 0.3 reduce_sum.103
  458.8 2.0 multiply_subtract_fusion
  (22 shorter events, 0.4 us)
Async XLA Ops:
  7.2 37.7 %copy-start = (bf16[4,112,896]{2,1,0:T(8,128)(2,1)S(1)}, bf16[4,112,896]{2,1,0:T(8,128)(2,1)}, u32[]{:S(2)}) copy-start(bf16[4,112,896]{2,1,0:T(8,128)(2,1)} %param.3) | copy-start | bytes 2408452
  7.2 37.7 %all-gather.4.cloned.1.call-start = ((), (), s32[]{:S(2)}) async-start(), calls=%async_computation.4 | async-start | bytes 4128768 | tf_op jit(solution)/shard_map/all_gather | solution.py:40
  9.3 163.8 %reduce-scatter.3.cloned.1.call-start = ((), (), s32[]{:S(2)}) async-start(), calls=%async_computation.5 | async-start | bytes 16056320 | tf_op jit(solution)/shard_map/reduce_scatter | solution.py:13
  53.8 168.3 %reduce-scatter.5.cloned.1.call-start = ((), (), s32[]{:S(2)}) async-start(), calls=%async_computation.6 | async-start | bytes 3612672 | tf_op jit(solution)/shard_map/reduce_scatter | solution.py:13
  173.1 140.9 %all-gather.6.cloned.1.call-start = ((), (), s32[]{:S(2)}) async-start(), calls=%async_computation.7 | async-start | bytes 6623232 | tf_op jit(solution)/shard_map/all_gather | solution.py:58
  223.9 90.1 %copy-start.1 = (bf16[112,896]{1,0:T(8,128)(2,1)S(1)}, bf16[112,896]{1,0:T(8,128)(2,1)}, u32[]{:S(2)}) copy-start(bf16[112,896]{1,0:T(8,128)(2,1)} %get-tuple-element.13) | copy-start | bytes 602116
  223.9 205.8 %all-gather.8.cloned.1.call-start = ((), (), s32[]{:S(2)}) async-start(), calls=%async_computation.8 | async-start | bytes 6623232 | tf_op jit(solution)/shard_map/all_gather | solution.py:58
Sparse Core Ops, SparseCore 0:
  9.8 34.9 all-gather.3
  53.9 119.1 reduce-scatter.2
  175.6 46.4 reduce-scatter.4
  225.1 88.8 all-gather.5
  344.9 84.7 all-gather.7
where the time goes:
time: 468 us; the launch traced here: 467 us
  waiting for transfers between devices  366 us (78%)
  blocking collectives  43.1 us (9%)
  matrix products  23.4 us (5%)
  between operations  13.9 us (3%)
  local copies, waits for them, and re-layouts  11.4 us (2%)
  other arithmetic  9.11 us (2%)
    all_gather x2, waiting for transfers between devices, shards(): shard_piece = lax.all_gather(rounded, ROW, axis=0, tiled=True)  170 us
    reduce_scatter x2, waiting for transfers between devices, sum_by_axis(): so_far = lax.psum_scatter(so_far, axis, scatter_dimension=0, tiled=True)  161 us
    all_to_all x2, blocking collectives, sent_to_all(): return lax.all_to_all(copies, axis, split_axis=0, concat_axis=0, tiled=True)  43.1 us
    all_gather x1, waiting for transfers between devices, shards(): gram_slabs = lax.all_gather(grams, 'col', axis=2, tiled=True)  35.5 us
    dot_general x2, matrix products, shards(): jnp.dot(add_columns, shard_piece.astype(jnp.float32), precision=high)  14 us
  transfers between devices with their start and end apart: 5, of which 5 were waited for; matrix products, arithmetic and copies ran while one was open for 3% of the time, Pallas kernels for 0%

commit v1 on v0

v1 whole, which is shorter than its diff:
```python
import jax
import jax.numpy as jnp
from jax import lax
from jax.sharding import Mesh
from jax.sharding import PartitionSpec as P


F32, BF16 = jnp.float32, jnp.bfloat16


def shift(x, axis, by):
    size = lax.axis_size(axis)
    return lax.ppermute(x, axis, [(i, (i + by) % size) for i in range(size)])


def all_shifts(x, axis):
    return [x] + [shift(x, axis, by) for by in range(1, lax.axis_size(axis))]


def core_pair(x, axis):
    other = shift(x, "core", 1)
    first = lax.axis_index("core") == 0
    return jnp.concatenate(
        [jnp.where(first, x, other), jnp.where(first, other, x)], axis=axis
    )


def rolled(blocks, start):
    n = blocks.shape[0]
    return [
        lax.dynamic_index_in_dim(blocks, (start + i) % n, 0, keepdims=False) for i in range(n)
    ]


def y_sum(parts):
    return sum(all_shifts(parts, "y"))


def shards(grams, weights):
    y, z, x = (lax.axis_index(a) for a in ("y", "z", "x"))
    core = lax.axis_index("core")
    models, slab, _ = grams.shape
    ny, nz, nx = (lax.axis_size(a) for a in ("y", "z", "x"))
    cols = weights.shape[2]
    half = models // 2
    turn = (x - y) % nx

    w_slots = all_shifts(weights, "y")

    chip_gram = core_pair(grams, 2)
    wide = chip_gram.shape[2]
    mine = lax.dynamic_slice_in_dim(chip_gram, core * half, half, 0)
    total = jnp.sum(chip_gram.astype(F32), axis=0).astype(BF16)
    mine, total = lax.optimization_barrier((mine, total))
    mine = lax.ppermute(
        mine, ("y", "x"), [(a * nx + b, b * nx + a) for a in range(ny) for b in range(nx)]
    )
    mine = jnp.stack(all_shifts(mine, "x"))
    gram_slots = core_pair(mine, 1)
    gram_slots = rolled(gram_slots, turn)

    total = lax.all_gather(total, "z", axis=0, tiled=True)
    rows = total.shape[0]
    total = lax.dynamic_slice_in_dim(total, core * (rows // 2), rows // 2, 0)
    total = jnp.stack(all_shifts(total, "x"))
    total = core_pair(total, 1)
    total = jnp.concatenate(rolled(total, turn), axis=1)

    product = jnp.einsum(
        "mkc,mkr->cr",
        jnp.concatenate(w_slots, axis=0),
        jnp.concatenate(gram_slots, axis=0),
        preferred_element_type=F32,
    )
    row_of = lax.broadcasted_iota(jnp.int32, (slab, wide), 0) + z * slab
    on_diag = row_of == lax.broadcasted_iota(jnp.int32, (slab, wide), 1)
    diag_part = jnp.where(on_diag[None], gram_slots[0], jnp.zeros((), BF16))
    diag_product = jnp.einsum(
        "mkc,mkr->cr", weights, diag_part, preferred_element_type=F32
    )
    part = 0.9 * product + 0.1 * diag_product
    right_side = lax.psum_scatter(part, "z", scatter_dimension=0, tiled=True)
    total_diag = jnp.sum(diag_part.astype(F32), axis=(0, 1))
    total_diag = lax.all_gather(total_diag, "z")
    total_diag = jnp.sum(total_diag, axis=0)[None]
    diag_rest = 0.9 * (total_diag - lax.reduce_precision(total_diag, 8, 7)) + 0.1 * total_diag

    def apply(direction):
        rounded = lax.optimization_barrier(direction.astype(BF16))
        everyone = jnp.concatenate(all_shifts(rounded, "y"), axis=1)
        product = lax.dot_general(
            everyone, total, (((1,), (1,)), ((), ())), preferred_element_type=F32
        )
        return 0.9 * product + diag_rest * rounded.astype(F32)

    def sums(*pairs):
        return jnp.stack([jnp.sum(a * b, axis=1) for a, b in pairs])

    mapped = apply(right_side)
    norm, curvature, square = y_sum(
        sums((right_side, right_side), (right_side, mapped), (mapped, mapped))
    )
    step = norm / curvature
    norm_next = norm - 2.0 * step * curvature + step * step * square
    merged = step[:, None] * right_side
    residual = right_side - step[:, None] * mapped
    direction = residual + (norm_next / norm)[:, None] * right_side
    mapped = apply(direction)
    norm, curvature = y_sum(sums((residual, residual), (direction, mapped)))
    step = norm / curvature
    merged = merged + step[:, None] * direction
    residual = residual - step[:, None] * mapped

    sent = jnp.stack([merged, residual]).reshape(2, cols // nz, nz, slab)
    sent = sent.transpose(2, 0, 3, 1)
    got = lax.all_to_all(sent, "z", 0, 0, tiled=True)
    got = got.transpose(1, 2, 0, 3).reshape(2, slab, cols)
    return got[0], got[1]


def solution(mesh):
    torus = Mesh(mesh.devices.reshape(4, 8, 4, 2), ("y", "z", "x", "core"))
    spec_in = P(None, ("y", "z"), ("x", "core"))
    spec_out = P(("y", "z"), ("x", "core"))
    return jax.shard_map(
        shards,
        mesh=torus,
        in_specs=(spec_in, spec_in),
        out_specs=(spec_out, spec_out),
        check_vma=False,
    )
```

time: 468 us -> 254 us (0.54)
  waiting for transfers between devices: 366 us -> 113 us
  starting transfers between devices: 0.2 us -> 43.1 us
  matrix products: 23.4 us -> 12.5 us
  blocking collectives: 43.1 us -> 49.3 us
  local copies, waits for them, and re-layouts: 11.4 us -> 6.26 us
  other arithmetic: 9.11 us -> 13.9 us
    all_gather x3 -> x1, waiting for transfers between devices: 206 us -> 0.02 us  [shards(): total = lax.all_gather(total, 'z', axis=0, tiled=True)]
    reduce_scatter x2 -> x1, waiting for transfers between devices: 161 us -> 0.01 us  [shards(): right_side = lax.psum_scatter(part, 'z', scatter_dimension=0, tiled=True)]
    ppermute x0 -> x25, waiting for transfers between devices: none -> 113 us  [the longest x24 113 us: shift(): return lax.ppermute(x, axis, [(i, (i + by) % size) for i in range(size)])]
    ppermute x0 -> x25, starting transfers between devices: none -> 43 us  [the longest x24 42.3 us: shift(): return lax.ppermute(x, axis, [(i, (i + by) % size) for i in range(size)])]
    all_gather x0 -> x1, blocking collectives: none -> 27.5 us  [shards(): total_diag = lax.all_gather(total_diag, 'z')]
    all_to_all x2 -> x1, blocking collectives: 43.1 us -> 21.8 us  [shards(): got = lax.all_to_all(sent, 'z', 0, 0, tiled=True)]
    dot_general x4, matrix products: 23.4 us -> 12.5 us  [the longest x1 6.93 us: shards(): jnp.einsum('mkc,mkr->cr', jnp.concatenate(w_slots, axis=0), jnp.concatena...]
    select_n x0 -> x3, other arithmetic: none -> 5.98 us  [the longest x2 5.54 us: core_pair(): jnp.where(first, other, x)]
  transfers between devices with their start and end apart: 5 -> 27, of which waited for: 5 -> 22; matrix products, arithmetic and copies ran while one was open for 3% -> 8% of each run, Pallas kernels for 0% -> 0%
where the time goes in v1:
time: 254 us; the launch traced here: 253 us
  waiting for transfers between devices  113 us (44%)
  blocking collectives  49.3 us (19%)
  starting transfers between devices  43.1 us (17%)
  between operations  14.3 us (6%)
  other arithmetic  13.9 us (5%)
  matrix products  12.5 us (5%)
  local copies, waits for them, and re-layouts  6.26 us (2%)
    ppermute x24, waiting for transfers between devices, shift(): return lax.ppermute(x, axis, [(i, (i + by) % size) for i in range(size)])  113 us
    ppermute x24, starting transfers between devices, shift(): return lax.ppermute(x, axis, [(i, (i + by) % size) for i in range(size)])  42.3 us
    all_gather x1, blocking collectives, shards(): total_diag = lax.all_gather(total_diag, 'z')  27.5 us
    all_to_all x1, blocking collectives, shards(): got = lax.all_to_all(sent, 'z', 0, 0, tiled=True)  21.8 us
    dot_general x1, matrix products, shards(): jnp.einsum('mkc,mkr->cr', jnp.concatenate(w_slots, axis=0), jnp.concatena...  6.93 us
    select_n x2, other arithmetic, core_pair(): jnp.where(first, other, x)  5.54 us
  transfers between devices with their start and end apart: 27, of which 22 were waited for; matrix products, arithmetic and copies ran while one was open for 8% of the time, Pallas kernels for 0%

profile of v1, /device:TPU:32, one launch (start us, length us, event | category | flops | bytes accessed | tf_op | source)
XLA Modules:
  0.0 252.5 jit_solution(12770986388945964034)
XLA Ops:
  7.3 2.0 collective-permute-done.3
  12.2 27.2 %collective-permute-start.7 = (bf16[2,112,896]{2,1,0:T(8,128)(2,1)S(1)}, bf16[2,112,896]{2,1,0:T(8,128)(2,1)S(1)}, u32[]{:S(2)}, u32[]{:S(2)}) collective-permute-start(bf16[2,112,896]{2,1,0:T(8,128)(2,1)S(1)} %collective-permute-done.4), channel_id=1, source_target_pairs={{0,6},{2,0},{4,2},{6,4},{1,7},{3,1},{5,3},{7,5},{8,14},{10,8},{12,... | collective-permute-start | bytes 1204232 | tf_op jit(solution)/shard_map/ppermute | solution.py:13
  40.3 15.7 %collective-permute-done.7 = bf16[2,112,896]{2,1,0:T(8,128)(2,1)S(1)} collective-permute-done((bf16[2,112,896]{2,1,0:T(8,128)(2,1)S(1)}, bf16[2,112,896]{2,1,0:T(8,128)(2,1)S(1)}, u32[]{:S(2)}, u32[]{:S(2)}) %collective-permute-start.7) | collective-permute-done | bytes 401440 | tf_op jit(solution)/shard_map/ppermute | solution.py:13
  56.0 3.4 %collective-permute-done.5 = bf16[2,112,896]{2,1,0:T(8,128)(2,1)S(1)} collective-permute-done((bf16[2,112,896]{2,1,0:T(8,128)(2,1)S(1)}, bf16[2,112,896]{2,1,0:T(8,128)(2,1)S(1)}, u32[]{:S(2)}, u32[]{:S(2)}) %collective-permute-start.5) | collective-permute-done | bytes 401440 | tf_op jit(solution)/shard_map/ppermute | solution.py:13
  67.6 14.5 %collective-permute-done.2 = bf16[4,112,896]{2,1,0:T(8,128)(2,1)} collective-permute-done((bf16[4,112,896]{2,1,0:T(8,128)(2,1)}, bf16[4,112,896]{2,1,0:T(8,128)(2,1)}, u32[]{:S(2)}, u32[]{:S(2)}) %collective-permute-start.2) | collective-permute-done | bytes 802848 | tf_op jit(solution)/shard_map/ppermute | solution.py:13
  82.1 2.6 %collective-permute-done.1 = bf16[4,112,896]{2,1,0:T(8,128)(2,1)} collective-permute-done((bf16[4,112,896]{2,1,0:T(8,128)(2,1)}, bf16[4,112,896]{2,1,0:T(8,128)(2,1)}, u32[]{:S(2)}, u32[]{:S(2)}) %collective-permute-start.1) | collective-permute-done | bytes 802848 | tf_op jit(solution)/shard_map/ppermute | solution.py:13
  84.7 16.4 %collective-permute-done = bf16[4,112,896]{2,1,0:T(8,128)(2,1)} collective-permute-done((bf16[4,112,896]{2,1,0:T(8,128)(2,1)}, bf16[4,112,896]{2,1,0:T(8,128)(2,1)}, u32[]{:S(2)}, u32[]{:S(2)}) %collective-permute-start) | collective-permute-done | bytes 802848 | tf_op jit(solution)/shard_map/ppermute | solution.py:13
  101.1 6.9 %bitcast_add_fusion = f32[896,896]{1,0:T(8,128)} fusion(f32[896,896,1]{0,1,2:T(8,128)S(1)} %fusion.52, bf16[4,112,896]{2,1,0:T(8,128)(2,1)S(1)} %get-tuple-element.25, bf16[4,112,896]{2,1,0:T(8,128)(2,1)S(1)} %get-tuple-element.24, bf16[4,112,896]{2,1,0:T(8,128)(2,1)S(1)} %get-tuple-element.23, bf16[4,112,896]{2,1,0:T(8,128)(2,1)S(1)} %get-tuple-element.16, ...), kind=kOutput, calls=%fused_computation.33 | convolution fusion | flops 2889334784 | bytes 12845056 | tf_op jit(solution)/shard_map/mkc,mkr->cr/dot_general | solution.py:69
  112.6 17.5 %collective-permute-done.14 = bf16[448,896]{1,0:T(8,128)(2,1)S(1)} collective-permute-done((bf16[448,896]{1,0:T(8,128)(2,1)S(1)}, bf16[448,896]{1,0:T(8,128)(2,1)S(1)}, u32[]{:S(2)}, u32[]{:S(2)}) %collective-permute-start.14) | collective-permute-done | bytes 802848 | tf_op jit(solution)/shard_map/ppermute | solution.py:13
  130.2 2.6 %collective-permute-done.13 = bf16[448,896]{1,0:T(8,128)(2,1)S(1)} collective-permute-done((bf16[448,896]{1,0:T(8,128)(2,1)S(1)}, bf16[448,896]{1,0:T(8,128)(2,1)S(1)}, u32[]{:S(2)}, u32[]{:S(2)}) %collective-permute-start.13) | collective-permute-done | bytes 802848 | tf_op jit(solution)/shard_map/ppermute | solution.py:13
  132.7 15.8 %collective-permute-done.12 = bf16[448,896]{1,0:T(8,128)(2,1)S(1)} collective-permute-done((bf16[448,896]{1,0:T(8,128)(2,1)S(1)}, bf16[448,896]{1,0:T(8,128)(2,1)S(1)}, u32[]{:S(2)}, u32[]{:S(2)}) %collective-permute-start.12) | collective-permute-done | bytes 802848 | tf_op jit(solution)/shard_map/ppermute | solution.py:13
  149.4 27.5 %all-gather.1 = f32[8,1,896]{2,1,0:T(1,128)S(1)} all-gather(f32[1,1,896]{2,1,0:T(1,128)S(1)} %reshape.85), channel_id=2, replica_groups=mesh['y'=4,'z'=8,'x'=4,'core'=2] {'z'}, dimensions={0}, use_global_device_ids=true | all-gather | bytes 32256 | tf_op jit(solution)/shard_map/all_gather | solution.py:84
  176.9 4.5 %broadcast_select_fusion = (bf16[4,448,896]{2,1,0:T(8,128)(2,1)S(1)}, bf16[4,448,896]{2,1,0:T(8,128)(2,1)}) fusion(bf16[4,448,896]{2,1,0:T(8,128)(2,1)} %collective-permute-done.15, pred[]{:T(512)S(6)} %eq.22, bf16[1,448,896]{2,1,0:T(8,128)(2,1)} %bitcast.69, bf16[1,448,896]{2,1,0:T(8,128)(2,1)} %bitcast.71, bf16[1,448,896]{2,1,0:T(8,128)(2,1)} %bitcast.73, ...), kind=kLoop, calls=%fused_computation.36 | loop fusion | flops 8028160 | bytes 12845057 | tf_op jit(solution)/shard_map/jit(_where)/select_n | solution.py:24
  184.5 2.7 %fusion.22 = (bf16[896,896]{1,0:T(8,128)(2,1)S(1)}, bf16[896,896]{1,0:T(8,128)(2,1)S(1)}, bf16[896,896]{1,0:T(8,128)(2,1)S(1)}, bf16[896,896]{1,0:T(8,128)(2,1)S(1)}) fusion(s32[]{:T(128)S(6)} %select_n.104, bf16[4,448,896]{2,1,0:T(8,128)(2,1)} %get-tuple-element.22, bf16[4,448,896]{2,1,0:T(8,128)(2,1)S(1)} %get-tuple-element.21, s32[]{:T(128)S(6)} %select_n.106, ...), kind=kLoop, calls=%fused_computation.41 | loop fusion | flops 12845056 | bytes 12845072 | tf_op jit(solution)/shard_map/jit(dynamic_index_in_dim)/squeeze | solution.py:31
  190.0 2.1 collective-permute-done.9
  192.1 2.2 multiply_reduce_fusion.4
  197.9 2.5 %collective-permute-done.17 = f32[3,112]{1,0:T(4,128)S(1)} collective-permute-done((f32[3,112]{1,0:T(4,128)S(1)}, f32[3,112]{1,0:T(4,128)S(1)}, u32[]{:S(2)}, u32[]{:S(2)}) %collective-permute-start.17) | collective-permute-done | bytes 1376 | tf_op jit(solution)/shard_map/ppermute | solution.py:13
  201.1 1.8 collective-permute-start.21
  204.2 2.7 %collective-permute-done.21 = bf16[112,896]{1,0:T(8,128)(2,1)S(1)} collective-permute-done((bf16[112,896]{1,0:T(8,128)(2,1)S(1)}, bf16[112,896]{1,0:T(8,128)(2,1)S(1)}, u32[]{:S(2)}, u32[]{:S(2)}) %collective-permute-start.21) | collective-permute-done | bytes 200736 | tf_op jit(solution)/shard_map/ppermute | solution.py:13
  206.9 3.3 %collective-permute-done.20 = bf16[112,896]{1,0:T(8,128)(2,1)S(1)} collective-permute-done((bf16[112,896]{1,0:T(8,128)(2,1)S(1)}, bf16[112,896]{1,0:T(8,128)(2,1)S(1)}, u32[]{:S(2)}, u32[]{:S(2)}) %collective-permute-start.20) | collective-permute-done | bytes 200736 | tf_op jit(solution)/shard_map/ppermute | solution.py:13
  210.2 2.1 collective-permute-done.19
  212.3 2.2 multiply_reduce_fusion.1
  218.2 2.1 collective-permute-done.23
  221.9 21.8 %all_to_all.5 = f32[8,2,112,112]{2,3,1,0:T(8,128)S(1)} all-to-all(f32[8,2,112,112]{2,3,1,0:T(8,128)S(1)} %maximum_bitcast_fusion), channel_id=1, replica_groups=mesh['y'=4,'z'=8,'x'=4,'core'=2] {'z'}, dimensions={0} | all-to-all | bytes 1605632 | tf_op jit(solution)/shard_map/all_to_all | solution.py:116
  (84 shorter events, 36.1 us)
Async XLA Ops:
  7.2 100.9 %all-gather.4.cloned.1.call-start = ((), (), s32[]{:S(2)}) async-start(), calls=%async_computation.3 | async-start | bytes 1806336 | tf_op jit(solution)/shard_map/all_gather | solution.py:62
  12.2 43.8 %collective-permute-start.7 = (bf16[2,112,896]{2,1,0:T(8,128)(2,1)S(1)}, bf16[2,112,896]{2,1,0:T(8,128)(2,1)S(1)}, u32[]{:S(2)}, u32[]{:S(2)}) collective-permute-start(bf16[2,112,896]{2,1,0:T(8,128)(2,1)S(1)} %collective-permute-done.4), channel_id=1, source_target_pairs={{0,6},{2,0},{4,2},{6,4},{1,7},{3,1},{5,3},{7,5},{8,14},{10,8},{12,... | collective-permute-start | bytes 1204232 | tf_op jit(solution)/shard_map/ppermute | solution.py:13
  39.4 16.6 %collective-permute-start.6 = (bf16[2,112,896]{2,1,0:T(8,128)(2,1)S(1)}, bf16[2,112,896]{2,1,0:T(8,128)(2,1)S(1)}, u32[]{:S(2)}, u32[]{:S(2)}) collective-permute-start(bf16[2,112,896]{2,1,0:T(8,128)(2,1)S(1)} %collective-permute-done.4), channel_id=1, source_target_pairs={{0,4},{2,6},{4,0},{6,2},{1,5},{3,7},{5,1},{7,3},{8,12},{10,14},{12... | collective-permute-start | bytes 1204232 | tf_op jit(solution)/shard_map/ppermute | solution.py:13
  39.4 20.0 %collective-permute-start.5 = (bf16[2,112,896]{2,1,0:T(8,128)(2,1)S(1)}, bf16[2,112,896]{2,1,0:T(8,128)(2,1)S(1)}, u32[]{:S(2)}, u32[]{:S(2)}) collective-permute-start(bf16[2,112,896]{2,1,0:T(8,128)(2,1)S(1)} %collective-permute-done.4), channel_id=1, source_target_pairs={{0,2},{2,4},{4,6},{6,0},{1,3},{3,5},{5,7},{7,1},{8,10},{10,12},{12... | collective-permute-start | bytes 1204232 | tf_op jit(solution)/shard_map/ppermute | solution.py:13
  60.8 3.7 %collective-permute-start.8 = (bf16[4,2,112,896]{3,2,1,0:T(8,128)(2,1)}, bf16[4,2,112,896]{3,2,1,0:T(8,128)(2,1)S(1)}, u32[]{:S(2)}, u32[]{:S(2)}) collective-permute-start(bf16[4,2,112,896]{3,2,1,0:T(8,128)(2,1)} %pad_maximum_fusion.2), channel_id=1, source_target_pairs={{0,1},{1,0},{2,3},{3,2},{4,5},{5,4},{6,7},{7,6},{8,9},{9,8},{10,11... | collective-permute-start | bytes 4816904 | tf_op jit(solution)/shard_map/ppermute | solution.py:13
  60.9 120.5 %reduce-scatter.2.cloned.1.call-start = ((), (), s32[]{:S(2)}) async-start(), calls=%async_computation.2 | async-start | bytes 3612672 | tf_op jit(solution)/shard_map/reduce_scatter | solution.py:82
  60.9 21.2 %collective-permute-start.2 = (bf16[4,112,896]{2,1,0:T(8,128)(2,1)}, bf16[4,112,896]{2,1,0:T(8,128)(2,1)}, u32[]{:S(2)}, u32[]{:S(2)}) collective-permute-start(bf16[4,112,896]{2,1,0:T(8,128)(2,1)} %param.3), channel_id=1, source_target_pairs={{0,192},{64,0},{128,64},{192,128},{1,193},{65,1},{129,65},{193,129... | collective-permute-start | bytes 2408456 | tf_op jit(solution)/shard_map/ppermute | solution.py:13
  62.1 22.6 %collective-permute-start.1 = (bf16[4,112,896]{2,1,0:T(8,128)(2,1)}, bf16[4,112,896]{2,1,0:T(8,128)(2,1)}, u32[]{:S(2)}, u32[]{:S(2)}) collective-permute-start(bf16[4,112,896]{2,1,0:T(8,128)(2,1)} %param.3), channel_id=1, source_target_pairs={{0,128},{64,192},{128,0},{192,64},{1,129},{65,193},{129,1},{193,65... | collective-permute-start | bytes 2408456 | tf_op jit(solution)/shard_map/ppermute | solution.py:13
  62.1 39.0 %collective-permute-start = (bf16[4,112,896]{2,1,0:T(8,128)(2,1)}, bf16[4,112,896]{2,1,0:T(8,128)(2,1)}, u32[]{:S(2)}, u32[]{:S(2)}) collective-permute-start(bf16[4,112,896]{2,1,0:T(8,128)(2,1)} %param.3), channel_id=1, source_target_pairs={{0,64},{64,128},{128,192},{192,0},{1,65},{65,129},{129,193},{193,1... | collective-permute-start | bytes 2408456 | tf_op jit(solution)/shard_map/ppermute | solution.py:13
  109.3 20.8 %collective-permute-start.14 = (bf16[448,896]{1,0:T(8,128)(2,1)S(1)}, bf16[448,896]{1,0:T(8,128)(2,1)S(1)}, u32[]{:S(2)}, u32[]{:S(2)}) collective-permute-start(bf16[448,896]{1,0:T(8,128)(2,1)S(1)} %constant_dynamic-slice_fusion), channel_id=1, source_target_pairs={{0,6},{2,0},{4,2},{6,4},{1,7},{3,1},{5,3},{7,5},{8,14},{10,8},{12,... | collective-permute-start | bytes 2408456 | tf_op jit(solution)/shard_map/ppermute | solution.py:13
  110.4 22.3 %collective-permute-start.13 = (bf16[448,896]{1,0:T(8,128)(2,1)S(1)}, bf16[448,896]{1,0:T(8,128)(2,1)S(1)}, u32[]{:S(2)}, u32[]{:S(2)}) collective-permute-start(bf16[448,896]{1,0:T(8,128)(2,1)S(1)} %constant_dynamic-slice_fusion), channel_id=1, source_target_pairs={{0,4},{2,6},{4,0},{6,2},{1,5},{3,7},{5,1},{7,3},{8,12},{10,14},{12... | collective-permute-start | bytes 2408456 | tf_op jit(solution)/shard_map/ppermute | solution.py:13
  110.4 38.1 %collective-permute-start.12 = (bf16[448,896]{1,0:T(8,128)(2,1)S(1)}, bf16[448,896]{1,0:T(8,128)(2,1)S(1)}, u32[]{:S(2)}, u32[]{:S(2)}) collective-permute-start(bf16[448,896]{1,0:T(8,128)(2,1)S(1)} %constant_dynamic-slice_fusion), channel_id=1, source_target_pairs={{0,2},{2,4},{4,6},{6,0},{1,3},{3,5},{5,7},{7,1},{8,10},{10,12},{12... | collective-permute-start | bytes 2408456 | tf_op jit(solution)/shard_map/ppermute | solution.py:13
  149.4 27.5 %collective-permute-start.15 = (bf16[4,448,896]{2,1,0:T(8,128)(2,1)S(1)}, bf16[4,448,896]{2,1,0:T(8,128)(2,1)}, u32[]{:S(2)}, u32[]{:S(2)}) collective-permute-start(bf16[4,448,896]{2,1,0:T(8,128)(2,1)S(1)} %pad_maximum_fusion.1), channel_id=1, source_target_pairs={{0,1},{1,0},{2,3},{3,2},{4,5},{5,4},{6,7},{7,6},{8,9},{9,8},{10,11... | collective-permute-start | bytes 9633800 | tf_op jit(solution)/shard_map/ppermute | solution.py:13
  182.4 5.8 %collective-permute-start.11 = (bf16[112,896]{1,0:T(8,128)(2,1)S(1)}, bf16[112,896]{1,0:T(8,128)(2,1)S(1)}, u32[]{:S(2)}, u32[]{:S(2)}) collective-permute-start(bf16[112,896]{1,0:T(8,128)(2,1)S(1)} %convert_element_type.17), channel_id=1, source_target_pairs={{0,192},{64,0},{128,64},{192,128},{1,193},{65,1},{129,65},{193,129... | collective-permute-start | bytes 602120 | tf_op jit(solution)/shard_map/ppermute | solution.py:13
  182.7 7.3 %collective-permute-start.10 = (bf16[112,896]{1,0:T(8,128)(2,1)S(1)}, bf16[112,896]{1,0:T(8,128)(2,1)S(1)}, u32[]{:S(2)}, u32[]{:S(2)}) collective-permute-start(bf16[112,896]{1,0:T(8,128)(2,1)S(1)} %convert_element_type.17), channel_id=1, source_target_pairs={{0,128},{64,192},{128,0},{192,64},{1,129},{65,193},{129,1},{193,65... | collective-permute-start | bytes 602120 | tf_op jit(solution)/shard_map/ppermute | solution.py:13
  183.3 8.7 %collective-permute-start.9 = (bf16[112,896]{1,0:T(8,128)(2,1)S(1)}, bf16[112,896]{1,0:T(8,128)(2,1)S(1)}, u32[]{:S(2)}, u32[]{:S(2)}) collective-permute-start(bf16[112,896]{1,0:T(8,128)(2,1)S(1)} %convert_element_type.17), channel_id=1, source_target_pairs={{0,64},{64,128},{128,192},{192,0},{1,65},{65,129},{129,193},{193,1... | collective-permute-start | bytes 602120 | tf_op jit(solution)/shard_map/ppermute | solution.py:13
  194.3 3.7 %collective-permute-start.18 = (f32[3,112]{1,0:T(4,128)S(1)}, f32[3,112]{1,0:T(4,128)S(1)}, u32[]{:S(2)}, u32[]{:S(2)}) collective-permute-start(f32[3,112]{1,0:T(4,128)S(1)} %pad_maximum_fusion.6), channel_id=1, source_target_pairs={{0,192},{64,0},{128,64},{192,128},{1,193},{65,1},{129,65},{193,129... | collective-permute-start | bytes 4040 | tf_op jit(solution)/shard_map/ppermute | solution.py:13
  195.4 5.1 %collective-permute-start.17 = (f32[3,112]{1,0:T(4,128)S(1)}, f32[3,112]{1,0:T(4,128)S(1)}, u32[]{:S(2)}, u32[]{:S(2)}) collective-permute-start(f32[3,112]{1,0:T(4,128)S(1)} %pad_maximum_fusion.6), channel_id=1, source_target_pairs={{0,128},{64,192},{128,0},{192,64},{1,129},{65,193},{129,1},{193,65... | collective-permute-start | bytes 4040 | tf_op jit(solution)/shard_map/ppermute | solution.py:13
  196.1 4.8 %collective-permute-start.16 = (f32[3,112]{1,0:T(4,128)S(1)}, f32[3,112]{1,0:T(4,128)S(1)}, u32[]{:S(2)}, u32[]{:S(2)}) collective-permute-start(f32[3,112]{1,0:T(4,128)S(1)} %pad_maximum_fusion.6), channel_id=1, source_target_pairs={{0,64},{64,128},{128,192},{192,0},{1,65},{65,129},{129,193},{193,1... | collective-permute-start | bytes 4040 | tf_op jit(solution)/shard_map/ppermute | solution.py:13
  201.1 5.8 %collective-permute-start.21 = (bf16[112,896]{1,0:T(8,128)(2,1)S(1)}, bf16[112,896]{1,0:T(8,128)(2,1)S(1)}, u32[]{:S(2)}, u32[]{:S(2)}) collective-permute-start(bf16[112,896]{1,0:T(8,128)(2,1)S(1)} %fusion.55), channel_id=1, source_target_pairs={{0,192},{64,0},{128,64},{192,128},{1,193},{65,1},{129,65},{193,129... | collective-permute-start | bytes 602120 | tf_op jit(solution)/shard_map/ppermute | solution.py:13
  202.9 7.3 %collective-permute-start.20 = (bf16[112,896]{1,0:T(8,128)(2,1)S(1)}, bf16[112,896]{1,0:T(8,128)(2,1)S(1)}, u32[]{:S(2)}, u32[]{:S(2)}) collective-permute-start(bf16[112,896]{1,0:T(8,128)(2,1)S(1)} %fusion.55), channel_id=1, source_target_pairs={{0,128},{64,192},{128,0},{192,64},{1,129},{65,193},{129,1},{193,65... | collective-permute-start | bytes 602120 | tf_op jit(solution)/shard_map/ppermute | solution.py:13
  203.8 8.5 %collective-permute-start.19 = (bf16[112,896]{1,0:T(8,128)(2,1)S(1)}, bf16[112,896]{1,0:T(8,128)(2,1)S(1)}, u32[]{:S(2)}, u32[]{:S(2)}) collective-permute-start(bf16[112,896]{1,0:T(8,128)(2,1)S(1)} %fusion.55), channel_id=1, source_target_pairs={{0,64},{64,128},{128,192},{192,0},{1,65},{65,129},{129,193},{193,1... | collective-permute-start | bytes 602120 | tf_op jit(solution)/shard_map/ppermute | solution.py:13
  215.2 5.1 %collective-permute-start.23 = (f32[2,112]{1,0:T(2,128)S(1)}, f32[2,112]{1,0:T(2,128)S(1)}, u32[]{:S(2)}, u32[]{:S(2)}) collective-permute-start(f32[2,112]{1,0:T(2,128)S(1)} %pad_maximum_fusion.7), channel_id=1, source_target_pairs={{0,128},{64,192},{128,0},{192,64},{1,129},{65,193},{129,1},{193,65... | collective-permute-start | bytes 2696 | tf_op jit(solution)/shard_map/ppermute | solution.py:13
  216.1 4.8 %collective-permute-start.22 = (f32[2,112]{1,0:T(2,128)S(1)}, f32[2,112]{1,0:T(2,128)S(1)}, u32[]{:S(2)}, u32[]{:S(2)}) collective-permute-start(f32[2,112]{1,0:T(2,128)S(1)} %pad_maximum_fusion.7), channel_id=1, source_target_pairs={{0,64},{64,128},{128,192},{192,0},{1,65},{65,129},{129,193},{193,1... | collective-permute-start | bytes 2696 | tf_op jit(solution)/shard_map/ppermute | solution.py:13
  (9 other events, 87.6 us)
Sparse Core Ops, SparseCore 0:
  61.0 38.2 all-gather.3
  108.2 44.8 reduce-scatter.1

commit v2 on v1

--- a/solution.py
+++ b/solution.py
@@ -1,6 +1,8 @@
 import jax
 import jax.numpy as jnp
 from jax import lax
+from jax.experimental import pallas as pl
+from jax.experimental.pallas import tpu as pltpu
 from jax.sharding import Mesh
 from jax.sharding import PartitionSpec as P
 
@@ -34,6 +36,60 @@
 
 def y_sum(parts):
     return sum(all_shifts(parts, "y"))
+
+
+def ring_scatter(parts):
+    z, n = lax.axis_index("z"), lax.axis_size("z")
+    far = n // 2
+    rows = parts.shape[1]
+    mid = rows // 2
+
+    def part(dest):
+        return lax.dynamic_index_in_dim(parts, (z + dest) % n, 0, keepdims=False)
+
+    opposite = part(far)
+    down, up = shift(opposite[:mid], "z", -1), shift(opposite[mid:], "z", 1)
+    for hops in range(far - 1, 0, -1):
+        down, up = lax.optimization_barrier((down, up))
+        if hops == far - 1:
+            down = jnp.pad(down, ((0, rows - mid), (0, 0)))
+            up = jnp.pad(up, ((mid, 0), (0, 0)))
+        down = shift(part(-hops) + down, "z", -1)
+        up = shift(part(hops) + up, "z", 1)
+    return part(0) + down + up
+
+
+def in_row_order(ours, theirs, deep):
+    blocks, _, wide = ours.shape
+
+    def kernel(ours_ref, theirs_ref, out_ref, sems):
+        y, x, core = (lax.axis_index(a) for a in ("y", "x", "core"))
+        copies = []
+        for slot in range(blocks):
+            to = lax.rem(slot + y - x + blocks, blocks) * 2
+            for i, ref in enumerate((ours_ref, theirs_ref)):
+                half = core if i == 0 else 1 - core
+                copies.append(
+                    pltpu.make_async_copy(
+                        ref.at[slot, pl.ds(0, deep)],
+                        out_ref.at[to + half],
+                        sems.at[slot * 2 + i],
+                    )
+                )
+        for copy in copies:
+            copy.start()
+        for copy in copies:
+            copy.wait()
+
+    out = pl.pallas_call(
+        kernel,
+        out_shape=jax.ShapeDtypeStruct((2 * blocks, deep, wide), ours.dtype),
+        in_specs=[pl.BlockSpec(memory_space=pl.ANY)] * 2,
+        out_specs=pl.BlockSpec(memory_space=pltpu.VMEM),
+        scratch_shapes=[pltpu.SemaphoreType.DMA((2 * blocks,))],
+        name="in_row_order",
+    )(ours, theirs)
+    return out.reshape(2 * blocks * deep, wide)
 
 
 def shards(grams, weights):
@@ -50,21 +106,45 @@
     chip_gram = core_pair(grams, 2)
     wide = chip_gram.shape[2]
     mine = lax.dynamic_slice_in_dim(chip_gram, core * half, half, 0)
-    total = jnp.sum(chip_gram.astype(F32), axis=0).astype(BF16)
+
+    total = jnp.sum(grams.astype(F32), axis=0)
+    row_of = lax.broadcasted_iota(jnp.int32, (slab, wide), 0) + z * slab
+    on_diag = row_of == lax.broadcasted_iota(jnp.int32, (slab, wide), 1)
+    col_of = lax.broadcasted_iota(jnp.int32, total.shape, 1) + core * (wide // 2)
+    block_diag = (row_of[:, : wide // 2] == col_of) & (x == y)
+    diag = jnp.sum(jnp.where(block_diag, total, 0.0), axis=0)
+    high = lax.reduce_precision(diag, 8, 7)
+    middle = lax.reduce_precision(diag - high, 8, 7)
+    low = diag - high - middle
+    tail = jnp.concatenate([jnp.stack([high, middle, low]), jnp.zeros((5, wide // 2), F32)])
+    total = jnp.concatenate([total, tail], axis=0).astype(BF16)
     mine, total = lax.optimization_barrier((mine, total))
+
     mine = lax.ppermute(
         mine, ("y", "x"), [(a * nx + b, b * nx + a) for a in range(ny) for b in range(nx)]
     )
+    total = lax.all_gather(total, "z")
     mine = jnp.stack(all_shifts(mine, "x"))
     gram_slots = core_pair(mine, 1)
     gram_slots = rolled(gram_slots, turn)
 
-    total = lax.all_gather(total, "z", axis=0, tiled=True)
-    rows = total.shape[0]
-    total = lax.dynamic_slice_in_dim(total, core * (rows // 2), rows // 2, 0)
-    total = jnp.stack(all_shifts(total, "x"))
-    total = core_pair(total, 1)
-    total = jnp.concatenate(rolled(total, turn), axis=1)
+    tail = total[:, slab:].astype(F32).sum(axis=0)
+    blank = jnp.zeros_like(tail)
+    tail = jnp.concatenate(
+        [jnp.where(core == 0, tail, blank), jnp.where(core == 0, blank, tail)], axis=1
+    )
+    total = total[:, :slab].reshape(nz * slab, -1).T
+    deep = total.shape[0]
+    total = jnp.concatenate([total, tail.astype(BF16)], axis=0)
+    ours = jnp.stack(all_shifts(total, "x"))
+    theirs = shift(ours, "core", 1)
+    tail = sum(
+        lax.dynamic_index_in_dim(t, turn, 0, keepdims=False)[deep:].astype(F32)
+        for t in (ours, theirs)
+    )
+    total = in_row_order(ours, theirs, deep)
+    total_diag = jnp.sum(tail, axis=0)[None]
+    diag_rest = 0.9 * (total_diag - tail[:1]) + 0.1 * total_diag
 
     product = jnp.einsum(
         "mkc,mkr->cr",
@@ -72,25 +152,17 @@
         jnp.concatenate(gram_slots, axis=0),
         preferred_element_type=F32,
     )
-    row_of = lax.broadcasted_iota(jnp.int32, (slab, wide), 0) + z * slab
-    on_diag = row_of == lax.broadcasted_iota(jnp.int32, (slab, wide), 1)
     diag_part = jnp.where(on_diag[None], gram_slots[0], jnp.zeros((), BF16))
     diag_product = jnp.einsum(
         "mkc,mkr->cr", weights, diag_part, preferred_element_type=F32
     )
     part = 0.9 * product + 0.1 * diag_product
-    right_side = lax.psum_scatter(part, "z", scatter_dimension=0, tiled=True)
-    total_diag = jnp.sum(diag_part.astype(F32), axis=(0, 1))
-    total_diag = lax.all_gather(total_diag, "z")
-    total_diag = jnp.sum(total_diag, axis=0)[None]
-    diag_rest = 0.9 * (total_diag - lax.reduce_precision(total_diag, 8, 7)) + 0.1 * total_diag
+    right_side = ring_scatter(part.reshape(nz, cols // nz, -1))
 
     def apply(direction):
         rounded = lax.optimization_barrier(direction.astype(BF16))
         everyone = jnp.concatenate(all_shifts(rounded, "y"), axis=1)
-        product = lax.dot_general(
-            everyone, total, (((1,), (1,)), ((), ())), preferred_element_type=F32
-        )
+        product = jnp.dot(everyone, total, preferred_element_type=F32)
         return 0.9 * product + diag_rest * rounded.astype(F32)
 
     def sums(*pairs):

time: 254 us -> 266 us (1.047)
  the two profiles are of different devices: /device:TPU:32 before, /device:TPU:2 now
where the time goes in v2:
time: 266 us; the launch traced here: 265 us
  waiting for transfers between devices  127 us (48%)
  blocking collectives  53.5 us (20%)
  starting transfers between devices  41.1 us (15%)
  other arithmetic  19.3 us (7%)
  matrix products  11.7 us (4%)
  local copies, waits for them, and re-layouts  5.83 us (2%)
  Pallas kernels  5.6 us (2%)
    ppermute x32, waiting for transfers between devices, shift(): return lax.ppermute(x, axis, [(i, (i + by) % size) for i in range(size)])  110 us
    ppermute x32, starting transfers between devices, shift(): return lax.ppermute(x, axis, [(i, (i + by) % size) for i in range(size)])  37.6 us
    all_gather x1, blocking collectives, shards(): total = lax.all_gather(total, 'z')  30.4 us
    all_to_all x1, blocking collectives, shards(): got = lax.all_to_all(sent, 'z', 0, 0, tiled=True)  23.1 us
    ppermute x1, waiting for transfers between devices, shards(): lax.ppermute(mine, ('y', 'x'), [(a * nx + b, b * nx + a) for a in range(n...  16.9 us
    dot_general x2, matrix products, apply(): product = jnp.dot(everyone, total, preferred_element_type=F32)  5.69 us
    pallas_call x1, Pallas kernels, in_row_order(): pl.pallas_call(kernel, out_shape=jax.ShapeDtypeStruct((2 * blocks, deep,...  5.6 us
  transfers between devices with their start and end apart: 33, of which 21 were waited for; matrix products, arithmetic and copies ran while one was open for 9% of the time, Pallas kernels for 2%

profile of v2, /device:TPU:2, one launch (start us, length us, event | category | flops | bytes accessed | tf_op | source)
XLA Modules:
  0.0 265.2 jit_solution(4021958764795308928)
XLA Ops:
  4.0 3.5 %collective-permute-start.4 = (bf16[2,112,896]{2,1,0:T(8,128)(2,1)S(1)}, bf16[2,112,896]{2,1,0:T(8,128)(2,1)S(1)}, u32[]{:S(2)}, u32[]{:S(2)}) collective-permute-start(bf16[2,112,896]{2,1,0:T(8,128)(2,1)S(1)} %fusion.46), channel_id=1, source_target_pairs={{0,0},{2,64},{4,128},{6,192},{64,2},{66,66},{68,130},{70,194},{128... | collective-permute-start | bytes 1204232 | tf_op jit(solution)/shard_map/ppermute | solution.py:123
  7.4 16.9 %collective-permute-done.4 = bf16[2,112,896]{2,1,0:T(8,128)(2,1)S(1)} collective-permute-done((bf16[2,112,896]{2,1,0:T(8,128)(2,1)S(1)}, bf16[2,112,896]{2,1,0:T(8,128)(2,1)S(1)}, u32[]{:S(2)}, u32[]{:S(2)}) %collective-permute-start.4) | collective-permute-done | bytes 401440 | tf_op jit(solution)/shard_map/ppermute | solution.py:123
  24.4 6.9 %collective-permute-start.6 = (bf16[2,112,896]{2,1,0:T(8,128)(2,1)S(1)}, bf16[2,112,896]{2,1,0:T(8,128)(2,1)S(1)}, u32[]{:S(2)}, u32[]{:S(2)}) collective-permute-start(bf16[2,112,896]{2,1,0:T(8,128)(2,1)S(1)} %collective-permute-done.4), channel_id=1, source_target_pairs={{0,4},{2,6},{4,0},{6,2},{1,5},{3,7},{5,1},{7,3},{8,12},{10,14},{12... | collective-permute-start | bytes 1204232 | tf_op jit(solution)/shard_map/ppermute | solution.py:15
  31.3 2.6 collective-permute-start.5
  34.0 30.4 %all-gather.1 = bf16[8,120,448]{1,2,0:T(8,128)(2,1)S(1)} all-gather(bf16[1,120,448]{1,2,0:T(8,128)(2,1)S(1)} %bitcast.121), channel_id=2, replica_groups=mesh['y'=4,'z'=8,'x'=4,'core'=2] {'z'}, dimensions={0}, use_global_device_ids=true | all-gather | bytes 967680 | tf_op jit(solution)/shard_map/all_gather | solution.py:126
  73.6 33.4 %collective-permute-done.22 = bf16[456,896]{1,0:T(8,128)(2,1)S(1)} collective-permute-done((bf16[456,896]{1,0:T(8,128)(2,1)}, bf16[456,896]{1,0:T(8,128)(2,1)S(1)}, u32[]{:S(2)}, u32[]{:S(2)}) %collective-permute-start.22) | collective-permute-done | bytes 817184 | tf_op jit(solution)/shard_map/ppermute | solution.py:15
  108.9 3.1 %pad_maximum_fusion.ours_ref = bf16[4,456,896]{2,1,0:T(8,128)(2,1)} fusion(bf16[1,456,896]{2,1,0:T(8,128)(2,1)S(1)} %bitcast.120, bf16[1,456,896]{2,1,0:T(8,128)(2,1)} %bitcast.27, bf16[1,456,896]{2,1,0:T(8,128)(2,1)} %bitcast.26, bf16[1,456,896]{2,1,0:T(8,128)(2,1)S(1)} %fusion.70), kind=kLoop, calls=%fused_computation.8 | loop fusion | flops 4902912 | bytes 6537216 | tf_op jit(solution)/shard_map/stack | solution.py:139
  116.2 13.3 %collective-permute-done.1 = bf16[4,112,896]{2,1,0:T(8,128)(2,1)S(1)} collective-permute-done((bf16[4,112,896]{2,1,0:T(8,128)(2,1)}, bf16[4,112,896]{2,1,0:T(8,128)(2,1)S(1)}, u32[]{:S(2)}, u32[]{:S(2)}) %collective-permute-start.1) | collective-permute-done | bytes 802848 | tf_op jit(solution)/shard_map/ppermute | solution.py:15
  129.5 15.7 %collective-permute-done = bf16[4,112,896]{2,1,0:T(8,128)(2,1)S(1)} collective-permute-done((bf16[4,112,896]{2,1,0:T(8,128)(2,1)}, bf16[4,112,896]{2,1,0:T(8,128)(2,1)S(1)}, u32[]{:S(2)}, u32[]{:S(2)}) %collective-permute-start) | collective-permute-done | bytes 802848 | tf_op jit(solution)/shard_map/ppermute | solution.py:15
  145.2 4.8 %bitcast_add_fusion = f32[896,896]{1,0:T(8,128)S(1)} fusion(f32[896,896,1]{0,1,2:T(8,128)S(1)} %fusion.43, bf16[4,112,896]{2,1,0:T(8,128)(2,1)S(1)} %get-tuple-element.42, bf16[4,112,896]{2,1,0:T(8,128)(2,1)S(1)} %get-tuple-element.41, bf16[4,112,896]{2,1,0:T(8,128)(2,1)S(1)} %get-tuple-element.39, bf16[4,112,896]{2,1,0:T(8,128)(2,1)S(1)} %get-tuple-element.40, ...), kind=kOutput, calls=%fused_computation.24 | convolution fusion | flops 2889334784 | bytes 12845056 | tf_op jit(solution)/shard_map/mkc,mkr->cr/dot_general | solution.py:149
  152.9 4.8 %collective-permute-done.9 = f32[56,896]{1,0:T(8,128)S(1)} collective-permute-done((f32[56,896]{1,0:T(8,128)}, f32[56,896]{1,0:T(8,128)S(1)}, u32[]{:S(2)}, u32[]{:S(2)}) %collective-permute-start.9) | collective-permute-done | bytes 200736 | tf_op jit(solution)/shard_map/ppermute | solution.py:15
  163.0 8.4 %collective-permute-done.11 = f32[112,896]{1,0:T(8,128)} collective-permute-done((f32[112,896]{1,0:T(8,128)}, f32[112,896]{1,0:T(8,128)}, u32[]{:S(2)}, u32[]{:S(2)}) %collective-permute-start.11) | collective-permute-done | bytes 401440 | tf_op jit(solution)/shard_map/ppermute | solution.py:15
  172.7 2.1 bitcast_add_fusion.2
  176.8 7.1 %collective-permute-done.13 = f32[112,896]{1,0:T(8,128)} collective-permute-done((f32[112,896]{1,0:T(8,128)}, f32[112,896]{1,0:T(8,128)}, u32[]{:S(2)}, u32[]{:S(2)}) %collective-permute-start.13) | collective-permute-done | bytes 401440 | tf_op jit(solution)/shard_map/ppermute | solution.py:15
  185.5 2.1 bitcast_add_fusion.6
  187.8 3.1 %collective-permute-start.15 = (f32[112,896]{1,0:T(8,128)}, f32[112,896]{1,0:T(8,128)S(1)}, u32[]{:S(2)}, u32[]{:S(2)}) collective-permute-start(f32[112,896]{1,0:T(8,128)} %get-tuple-element.31), channel_id=1, source_target_pairs={{0,56},{8,0},{16,8},{24,16},{32,24},{40,32},{48,40},{56,48},{1,57}... | collective-permute-start | bytes 1204232 | tf_op jit(solution)/shard_map/ppermute | solution.py:15
  190.9 6.2 %collective-permute-done.16 = f32[112,896]{1,0:T(8,128)S(1)} collective-permute-done((f32[112,896]{1,0:T(8,128)}, f32[112,896]{1,0:T(8,128)S(1)}, u32[]{:S(2)}, u32[]{:S(2)}) %collective-permute-start.16) | collective-permute-done | bytes 401440 | tf_op jit(solution)/shard_map/ppermute | solution.py:15
  201.6 5.6 %in_row_order.1 = bf16[8,448,896]{2,1,0:T(8,128)(2,1)} custom-call(bf16[4,456,896]{2,1,0:T(8,128)(2,1)} %pad_maximum_fusion.ours_ref, bf16[4,456,896]{2,1,0:T(8,128)(2,1)} %collective-permute-done.23.theirs_ref), custom_call_target="tpu_custom_call" | custom-call | tf_op jit(solution)/shard_map/in_row_order/pallas_call | solution.py:84
  208.0 4.4 %multiply_reduce_fusion.4 = (f32[112]{0:T(128)S(1)}, f32[112]{0:T(128)S(1)}, f32[112]{0:T(128)S(1)}, f32[112,896]{1,0:T(8,128)S(1)}) fusion(f32[112,896]{1,0:T(8,128)S(1)} %get-tuple-element.30, bf16[112,896]{1,0:T(8,128)(2,1)S(1)} %get-tuple-element.29, f32[896]{0:T(1024)S(1)} %fusion.53, bf16[3584,896]{1,0:T(8,128)(2,1)} %bitcast.102, ...), kind=kOutput, calls=%fused_computation.84 | convolution fusion | flops 723537536 | bytes 8033088 | tf_op jit(solution)/shard_map/dot_general | solution.py:165
  216.9 2.6 collective-permute-done.25
  224.0 3.2 %collective-permute-done.29 = bf16[112,896]{1,0:T(8,128)(2,1)S(1)} collective-permute-done((bf16[112,896]{1,0:T(8,128)(2,1)S(1)}, bf16[112,896]{1,0:T(8,128)(2,1)S(1)}, u32[]{:S(2)}, u32[]{:S(2)}) %collective-permute-start.29) | collective-permute-done | bytes 200736 | tf_op jit(solution)/shard_map/ppermute | solution.py:15
  228.9 2.1 collective-permute-done.27
  236.0 2.6 collective-permute-done.31
  240.1 23.1 %all_to_all.5 = f32[8,2,112,112]{2,3,1,0:T(8,128)S(1)} all-to-all(f32[8,2,112,112]{2,3,1,0:T(8,128)S(1)} %maximum_bitcast_fusion), channel_id=1, replica_groups=mesh['y'=4,'z'=8,'x'=4,'core'=2] {'z'}, dimensions={0} | all-to-all | bytes 1605632 | tf_op jit(solution)/shard_map/all_to_all | solution.py:188
  (100 shorter events, 56.4 us)
Async XLA Ops:
  4.0 20.4 %collective-permute-start.4 = (bf16[2,112,896]{2,1,0:T(8,128)(2,1)S(1)}, bf16[2,112,896]{2,1,0:T(8,128)(2,1)S(1)}, u32[]{:S(2)}, u32[]{:S(2)}) collective-permute-start(bf16[2,112,896]{2,1,0:T(8,128)(2,1)S(1)} %fusion.46), channel_id=1, source_target_pairs={{0,0},{2,64},{4,128},{6,192},{64,2},{66,66},{68,130},{70,194},{128... | collective-permute-start | bytes 1204232 | tf_op jit(solution)/shard_map/ppermute | solution.py:123
  24.3 40.1 %collective-permute-start.7 = (bf16[2,112,896]{2,1,0:T(8,128)(2,1)S(1)}, bf16[2,112,896]{2,1,0:T(8,128)(2,1)S(1)}, u32[]{:S(2)}, u32[]{:S(2)}) collective-permute-start(bf16[2,112,896]{2,1,0:T(8,128)(2,1)S(1)} %collective-permute-done.4), channel_id=1, source_target_pairs={{0,6},{2,0},{4,2},{6,4},{1,7},{3,1},{5,3},{7,5},{8,14},{10,8},{12,... | collective-permute-start | bytes 1204232 | tf_op jit(solution)/shard_map/ppermute | solution.py:15
  24.4 40.1 %collective-permute-start.6 = (bf16[2,112,896]{2,1,0:T(8,128)(2,1)S(1)}, bf16[2,112,896]{2,1,0:T(8,128)(2,1)S(1)}, u32[]{:S(2)}, u32[]{:S(2)}) collective-permute-start(bf16[2,112,896]{2,1,0:T(8,128)(2,1)S(1)} %collective-permute-done.4), channel_id=1, source_target_pairs={{0,4},{2,6},{4,0},{6,2},{1,5},{3,7},{5,1},{7,3},{8,12},{10,14},{12... | collective-permute-start | bytes 1204232 | tf_op jit(solution)/shard_map/ppermute | solution.py:15
  31.3 33.2 %collective-permute-start.5 = (bf16[2,112,896]{2,1,0:T(8,128)(2,1)S(1)}, bf16[2,112,896]{2,1,0:T(8,128)(2,1)S(1)}, u32[]{:S(2)}, u32[]{:S(2)}) collective-permute-start(bf16[2,112,896]{2,1,0:T(8,128)(2,1)S(1)} %collective-permute-done.4), channel_id=1, source_target_pairs={{0,2},{2,4},{4,6},{6,0},{1,3},{3,5},{5,7},{7,1},{8,10},{10,12},{12... | collective-permute-start | bytes 1204232 | tf_op jit(solution)/shard_map/ppermute | solution.py:15
  65.9 46.1 %collective-permute-start.8 = (bf16[4,2,112,896]{3,2,1,0:T(8,128)(2,1)}, bf16[4,2,112,896]{3,2,1,0:T(8,128)(2,1)}, u32[]{:S(2)}, u32[]{:S(2)}) collective-permute-start(bf16[4,2,112,896]{3,2,1,0:T(8,128)(2,1)} %pad_maximum_fusion.1), channel_id=1, source_target_pairs={{0,1},{1,0},{2,3},{3,2},{4,5},{5,4},{6,7},{7,6},{8,9},{9,8},{10,11... | collective-permute-start | bytes 4816904 | tf_op jit(solution)/shard_map/ppermute | solution.py:15
  68.7 38.3 %collective-permute-start.22 = (bf16[456,896]{1,0:T(8,128)(2,1)}, bf16[456,896]{1,0:T(8,128)(2,1)S(1)}, u32[]{:S(2)}, u32[]{:S(2)}) collective-permute-start(bf16[456,896]{1,0:T(8,128)(2,1)} %maximum_maximum_fusion), channel_id=1, source_target_pairs={{0,6},{2,0},{4,2},{6,4},{1,7},{3,1},{5,3},{7,5},{8,14},{10,8},{12,... | collective-permute-start | bytes 2451464 | tf_op jit(solution)/shard_map/ppermute | solution.py:15
  68.7 38.9 %collective-permute-start.21 = (bf16[456,896]{1,0:T(8,128)(2,1)}, bf16[456,896]{1,0:T(8,128)(2,1)}, u32[]{:S(2)}, u32[]{:S(2)}) collective-permute-start(bf16[456,896]{1,0:T(8,128)(2,1)} %maximum_maximum_fusion), channel_id=1, source_target_pairs={{0,4},{2,6},{4,0},{6,2},{1,5},{3,7},{5,1},{7,3},{8,12},{10,14},{12... | collective-permute-start | bytes 2451464 | tf_op jit(solution)/shard_map/ppermute | solution.py:15
  70.0 39.0 %collective-permute-start.20 = (bf16[456,896]{1,0:T(8,128)(2,1)}, bf16[456,896]{1,0:T(8,128)(2,1)}, u32[]{:S(2)}, u32[]{:S(2)}) collective-permute-start(bf16[456,896]{1,0:T(8,128)(2,1)} %maximum_maximum_fusion), channel_id=1, source_target_pairs={{0,2},{2,4},{4,6},{6,0},{1,3},{3,5},{5,7},{7,1},{8,10},{10,12},{12... | collective-permute-start | bytes 2451464 | tf_op jit(solution)/shard_map/ppermute | solution.py:15
  71.7 44.5 %collective-permute-start.2 = (bf16[4,112,896]{2,1,0:T(8,128)(2,1)}, bf16[4,112,896]{2,1,0:T(8,128)(2,1)}, u32[]{:S(2)}, u32[]{:S(2)}) collective-permute-start(bf16[4,112,896]{2,1,0:T(8,128)(2,1)} %param.3), channel_id=1, source_target_pairs={{0,192},{64,0},{128,64},{192,128},{1,193},{65,1},{129,65},{193,129... | collective-permute-start | bytes 2408456 | tf_op jit(solution)/shard_map/ppermute | solution.py:15
  107.0 22.5 %collective-permute-start.1 = (bf16[4,112,896]{2,1,0:T(8,128)(2,1)}, bf16[4,112,896]{2,1,0:T(8,128)(2,1)S(1)}, u32[]{:S(2)}, u32[]{:S(2)}) collective-permute-start(bf16[4,112,896]{2,1,0:T(8,128)(2,1)} %param.3), channel_id=1, source_target_pairs={{0,128},{64,192},{128,0},{192,64},{1,129},{65,193},{129,1},{193,65... | collective-permute-start | bytes 2408456 | tf_op jit(solution)/shard_map/ppermute | solution.py:15
  107.6 37.6 %collective-permute-start = (bf16[4,112,896]{2,1,0:T(8,128)(2,1)}, bf16[4,112,896]{2,1,0:T(8,128)(2,1)S(1)}, u32[]{:S(2)}, u32[]{:S(2)}) collective-permute-start(bf16[4,112,896]{2,1,0:T(8,128)(2,1)} %param.3), channel_id=1, source_target_pairs={{0,64},{64,128},{128,192},{192,0},{1,65},{65,129},{129,193},{193,1... | collective-permute-start | bytes 2408456 | tf_op jit(solution)/shard_map/ppermute | solution.py:15
  112.0 89.6 %collective-permute-start.23 = (bf16[4,456,896]{2,1,0:T(8,128)(2,1)}, bf16[4,456,896]{2,1,0:T(8,128)(2,1)}, u32[]{:S(2)}, u32[]{:S(2)}) collective-permute-start(bf16[4,456,896]{2,1,0:T(8,128)(2,1)} %pad_maximum_fusion.ours_ref), channel_id=1, source_target_pairs={{0,1},{1,0},{2,3},{3,2},{4,5},{5,4},{6,7},{7,6},{8,9},{9,8},{10,11... | collective-permute-start | bytes 9805832 | tf_op jit(solution)/shard_map/ppermute | solution.py:15
  150.9 8.1 %collective-permute-start.10 = (f32[56,896]{1,0:T(8,128)}, f32[56,896]{1,0:T(8,128)}, u32[]{:S(2)}, u32[]{:S(2)}) collective-permute-start(f32[56,896]{1,0:T(8,128)} %get-tuple-element.37), channel_id=1, source_target_pairs={{0,8},{8,16},{16,24},{24,32},{32,40},{40,48},{48,56},{56,0},{1,9},... | collective-permute-start | bytes 602120 | tf_op jit(solution)/shard_map/ppermute | solution.py:15
  161.0 10.4 %collective-permute-start.11 = (f32[112,896]{1,0:T(8,128)}, f32[112,896]{1,0:T(8,128)}, u32[]{:S(2)}, u32[]{:S(2)}) collective-permute-start(f32[112,896]{1,0:T(8,128)} %get-tuple-element.36), channel_id=1, source_target_pairs={{0,56},{8,0},{16,8},{24,16},{32,24},{40,32},{48,40},{56,48},{1,57}... | collective-permute-start | bytes 1204232 | tf_op jit(solution)/shard_map/ppermute | solution.py:15
  161.5 11.2 %collective-permute-start.12 = (f32[112,896]{1,0:T(8,128)}, f32[112,896]{1,0:T(8,128)}, u32[]{:S(2)}, u32[]{:S(2)}) collective-permute-start(f32[112,896]{1,0:T(8,128)} %get-tuple-element.35), channel_id=1, source_target_pairs={{0,8},{8,16},{16,24},{24,32},{32,40},{40,48},{48,56},{56,0},{1,9},... | collective-permute-start | bytes 1204232 | tf_op jit(solution)/shard_map/ppermute | solution.py:15
  174.8 9.2 %collective-permute-start.13 = (f32[112,896]{1,0:T(8,128)}, f32[112,896]{1,0:T(8,128)}, u32[]{:S(2)}, u32[]{:S(2)}) collective-permute-start(f32[112,896]{1,0:T(8,128)} %get-tuple-element.34), channel_id=1, source_target_pairs={{0,56},{8,0},{16,8},{24,16},{32,24},{40,32},{48,40},{56,48},{1,57}... | collective-permute-start | bytes 1204232 | tf_op jit(solution)/shard_map/ppermute | solution.py:15
  175.1 10.4 %collective-permute-start.14 = (f32[112,896]{1,0:T(8,128)}, f32[112,896]{1,0:T(8,128)}, u32[]{:S(2)}, u32[]{:S(2)}) collective-permute-start(f32[112,896]{1,0:T(8,128)} %get-tuple-element.33), channel_id=1, source_target_pairs={{0,8},{8,16},{16,24},{24,32},{32,40},{40,48},{48,56},{56,0},{1,9},... | collective-permute-start | bytes 1204232 | tf_op jit(solution)/shard_map/ppermute | solution.py:15
  187.6 9.4 %collective-permute-start.16 = (f32[112,896]{1,0:T(8,128)}, f32[112,896]{1,0:T(8,128)S(1)}, u32[]{:S(2)}, u32[]{:S(2)}) collective-permute-start(f32[112,896]{1,0:T(8,128)} %get-tuple-element.32), channel_id=1, source_target_pairs={{0,8},{8,16},{16,24},{24,32},{32,40},{40,48},{48,56},{56,0},{1,9},... | collective-permute-start | bytes 1204232 | tf_op jit(solution)/shard_map/ppermute | solution.py:15
  187.8 9.3 %collective-permute-start.15 = (f32[112,896]{1,0:T(8,128)}, f32[112,896]{1,0:T(8,128)S(1)}, u32[]{:S(2)}, u32[]{:S(2)}) collective-permute-start(f32[112,896]{1,0:T(8,128)} %get-tuple-element.31), channel_id=1, source_target_pairs={{0,56},{8,0},{16,8},{24,16},{32,24},{40,32},{48,40},{56,48},{1,57}... | collective-permute-start | bytes 1204232 | tf_op jit(solution)/shard_map/ppermute | solution.py:15
  198.1 9.9 %collective-permute-start.19 = (bf16[112,896]{1,0:T(8,128)(2,1)S(1)}, bf16[112,896]{1,0:T(8,128)(2,1)S(1)}, u32[]{:S(2)}, u32[]{:S(2)}) collective-permute-start(bf16[112,896]{1,0:T(8,128)(2,1)S(1)} %get-tuple-element.29), channel_id=1, source_target_pairs={{0,192},{64,0},{128,64},{192,128},{1,193},{65,1},{129,65},{193,129... | collective-permute-start | bytes 602120 | tf_op jit(solution)/shard_map/ppermute | solution.py:15
  198.4 9.6 %collective-permute-start.18 = (bf16[112,896]{1,0:T(8,128)(2,1)S(1)}, bf16[112,896]{1,0:T(8,128)(2,1)S(1)}, u32[]{:S(2)}, u32[]{:S(2)}) collective-permute-start(bf16[112,896]{1,0:T(8,128)(2,1)S(1)} %get-tuple-element.29), channel_id=1, source_target_pairs={{0,128},{64,192},{128,0},{192,64},{1,129},{65,193},{129,1},{193,65... | collective-permute-start | bytes 602120 | tf_op jit(solution)/shard_map/ppermute | solution.py:15
  200.3 7.7 %collective-permute-start.17 = (bf16[112,896]{1,0:T(8,128)(2,1)S(1)}, bf16[112,896]{1,0:T(8,128)(2,1)S(1)}, u32[]{:S(2)}, u32[]{:S(2)}) collective-permute-start(bf16[112,896]{1,0:T(8,128)(2,1)S(1)} %get-tuple-element.29), channel_id=1, source_target_pairs={{0,64},{64,128},{128,192},{192,0},{1,65},{65,129},{129,193},{193,1... | collective-permute-start | bytes 602120 | tf_op jit(solution)/shard_map/ppermute | solution.py:15
  221.5 7.4 %collective-permute-start.28 = (bf16[112,896]{1,0:T(8,128)(2,1)S(1)}, bf16[112,896]{1,0:T(8,128)(2,1)S(1)}, u32[]{:S(2)}, u32[]{:S(2)}) collective-permute-start(bf16[112,896]{1,0:T(8,128)(2,1)S(1)} %fusion.49), channel_id=1, source_target_pairs={{0,128},{64,192},{128,0},{192,64},{1,129},{65,193},{129,1},{193,65... | collective-permute-start | bytes 602120 | tf_op jit(solution)/shard_map/ppermute | solution.py:15
  222.9 8.1 %collective-permute-start.27 = (bf16[112,896]{1,0:T(8,128)(2,1)S(1)}, bf16[112,896]{1,0:T(8,128)(2,1)S(1)}, u32[]{:S(2)}, u32[]{:S(2)}) collective-permute-start(bf16[112,896]{1,0:T(8,128)(2,1)S(1)} %fusion.49), channel_id=1, source_target_pairs={{0,64},{64,128},{128,192},{192,0},{1,65},{65,129},{129,193},{193,1... | collective-permute-start | bytes 602120 | tf_op jit(solution)/shard_map/ppermute | solution.py:15
  (12 other events, 105.2 us)

commit v3 on v2

--- a/solution.py
+++ b/solution.py
@@ -123,7 +123,8 @@
     mine = lax.ppermute(
         mine, ("y", "x"), [(a * nx + b, b * nx + a) for a in range(ny) for b in range(nx)]
     )
-    total = lax.all_gather(total, "z")
+    total = jnp.broadcast_to(total, (nz, *total.shape))
+    total = lax.all_to_all(total, "z", 0, 0, tiled=True)
     mine = jnp.stack(all_shifts(mine, "x"))
     gram_slots = core_pair(mine, 1)
     gram_slots = rolled(gram_slots, turn)
@@ -183,11 +184,11 @@
     merged = merged + step[:, None] * direction
     residual = residual - step[:, None] * mapped
 
-    sent = jnp.stack([merged, residual]).reshape(2, cols // nz, nz, slab)
+    sent = jnp.stack([merged, residual]).astype(BF16).reshape(2, cols // nz, nz, slab)
     sent = sent.transpose(2, 0, 3, 1)
     got = lax.all_to_all(sent, "z", 0, 0, tiled=True)
     got = got.transpose(1, 2, 0, 3).reshape(2, slab, cols)
-    return got[0], got[1]
+    return got[0].astype(F32), got[1].astype(F32)
 
 
 def solution(mesh):

time: 266 us -> 242 us (0.910)
  the two profiles are of different devices: /device:TPU:2 before, /device:TPU:32 now
where the time goes in v3:
time: 242 us; the launch traced here: 241 us
  waiting for transfers between devices  116 us (48%)
  starting transfers between devices  61.8 us (26%)
  other arithmetic  19.1 us (8%)
  blocking collectives  18.8 us (8%)
  matrix products  11.6 us (5%)
  local copies, waits for them, and re-layouts  7.38 us (3%)
  Pallas kernels  5.62 us (2%)
    ppermute x32, waiting for transfers between devices, shift(): return lax.ppermute(x, axis, [(i, (i + by) % size) for i in range(size)])  116 us
    ppermute x32, starting transfers between devices, shift(): return lax.ppermute(x, axis, [(i, (i + by) % size) for i in range(size)])  52.5 us
    all_to_all x1, blocking collectives, shards(): got = lax.all_to_all(sent, 'z', 0, 0, tiled=True)  18.8 us
    all_to_all x1, starting transfers between devices, shards(): total = lax.all_to_all(total, 'z', 0, 0, tiled=True)  8.57 us
    dot_general x2, matrix products, apply(): product = jnp.dot(everyone, total, preferred_element_type=F32)  5.66 us
    pallas_call x1, Pallas kernels, in_row_order(): pl.pallas_call(kernel, out_shape=jax.ShapeDtypeStruct((2 * blocks, deep,...  5.62 us
  transfers between devices with their start and end apart: 34, of which 24 were waited for; matrix products, arithmetic and copies ran while one was open for 11% of the time, Pallas kernels for 2%

profile of v3, /device:TPU:32, one launch (start us, length us, event | category | flops | bytes accessed | tf_op | source)
XLA Modules:
  0.0 241.0 jit_solution(289517410402620569)
XLA Ops:
  5.2 8.6 %all-to-all-start = ((bf16[8,120,448]{1,2,0:T(8,128)(2,1)}), bf16[8,120,448]{1,2,0:T(8,128)(2,1)S(1)}, u32[]{:S(2)}, u32[]{:S(2)}) async-start(bf16[8,120,448]{1,2,0:T(8,128)(2,1)} %broadcast_in_dim.38), calls=%async_computation | async-start | bytes 1835008 | tf_op jit(solution)/shard_map/all_to_all | solution.py:127
  14.4 26.6 %collective-permute-start.7 = (bf16[2,112,896]{2,1,0:T(8,128)(2,1)S(1)}, bf16[2,112,896]{2,1,0:T(8,128)(2,1)S(1)}, u32[]{:S(2)}, u32[]{:S(2)}) collective-permute-start(bf16[2,112,896]{2,1,0:T(8,128)(2,1)S(1)} %collective-permute-done.4), channel_id=1, source_target_pairs={{0,6},{2,0},{4,2},{6,4},{1,7},{3,1},{5,3},{7,5},{8,14},{10,8},{12,... | collective-permute-start | bytes 1204232 | tf_op jit(solution)/shard_map/ppermute | solution.py:15
  42.0 15.2 %collective-permute-done.7 = bf16[2,112,896]{2,1,0:T(8,128)(2,1)S(1)} collective-permute-done((bf16[2,112,896]{2,1,0:T(8,128)(2,1)S(1)}, bf16[2,112,896]{2,1,0:T(8,128)(2,1)S(1)}, u32[]{:S(2)}, u32[]{:S(2)}) %collective-permute-start.7) | collective-permute-done | bytes 401440 | tf_op jit(solution)/shard_map/ppermute | solution.py:15
  57.1 3.4 %collective-permute-done.5 = bf16[2,112,896]{2,1,0:T(8,128)(2,1)S(1)} collective-permute-done((bf16[2,112,896]{2,1,0:T(8,128)(2,1)S(1)}, bf16[2,112,896]{2,1,0:T(8,128)(2,1)S(1)}, u32[]{:S(2)}, u32[]{:S(2)}) %collective-permute-start.5) | collective-permute-done | bytes 401440 | tf_op jit(solution)/shard_map/ppermute | solution.py:15
  68.9 17.4 %collective-permute-done.22 = bf16[456,896]{1,0:T(8,128)(2,1)S(1)} collective-permute-done((bf16[456,896]{1,0:T(8,128)(2,1)}, bf16[456,896]{1,0:T(8,128)(2,1)S(1)}, u32[]{:S(2)}, u32[]{:S(2)}) %collective-permute-start.22) | collective-permute-done | bytes 817184 | tf_op jit(solution)/shard_map/ppermute | solution.py:15
  86.3 2.5 %collective-permute-done.21 = bf16[456,896]{1,0:T(8,128)(2,1)} collective-permute-done((bf16[456,896]{1,0:T(8,128)(2,1)}, bf16[456,896]{1,0:T(8,128)(2,1)}, u32[]{:S(2)}, u32[]{:S(2)}) %collective-permute-start.21) | collective-permute-done | bytes 817184 | tf_op jit(solution)/shard_map/ppermute | solution.py:15
  88.9 16.7 %collective-permute-done.20 = bf16[456,896]{1,0:T(8,128)(2,1)} collective-permute-done((bf16[456,896]{1,0:T(8,128)(2,1)}, bf16[456,896]{1,0:T(8,128)(2,1)}, u32[]{:S(2)}, u32[]{:S(2)}) %collective-permute-start.20) | collective-permute-done | bytes 817184 | tf_op jit(solution)/shard_map/ppermute | solution.py:15
  105.6 3.1 %pad_maximum_fusion.ours_ref = bf16[4,456,896]{2,1,0:T(8,128)(2,1)} fusion(bf16[1,456,896]{2,1,0:T(8,128)(2,1)S(1)} %bitcast.121, bf16[1,456,896]{2,1,0:T(8,128)(2,1)} %bitcast.26, bf16[1,456,896]{2,1,0:T(8,128)(2,1)} %bitcast.25, bf16[1,456,896]{2,1,0:T(8,128)(2,1)S(1)} %fusion.70), kind=kLoop, calls=%fused_computation.8 | loop fusion | flops 4902912 | bytes 6537216 | tf_op jit(solution)/shard_map/stack | solution.py:140
  112.9 11.4 %collective-permute-done = bf16[4,112,896]{2,1,0:T(8,128)(2,1)S(1)} collective-permute-done((bf16[4,112,896]{2,1,0:T(8,128)(2,1)}, bf16[4,112,896]{2,1,0:T(8,128)(2,1)S(1)}, u32[]{:S(2)}, u32[]{:S(2)}) %collective-permute-start) | collective-permute-done | bytes 802848 | tf_op jit(solution)/shard_map/ppermute | solution.py:15
  124.3 4.8 %bitcast_add_fusion = f32[896,896]{1,0:T(8,128)S(1)} fusion(f32[896,896,1]{0,1,2:T(8,128)S(1)} %fusion.43, bf16[4,112,896]{2,1,0:T(8,128)(2,1)S(1)} %get-tuple-element.44, bf16[4,112,896]{2,1,0:T(8,128)(2,1)S(1)} %get-tuple-element.43, bf16[4,112,896]{2,1,0:T(8,128)(2,1)S(1)} %get-tuple-element.41, bf16[4,112,896]{2,1,0:T(8,128)(2,1)S(1)} %get-tuple-element.42, ...), kind=kOutput, calls=%fused_computation.24 | convolution fusion | flops 2889334784 | bytes 12845056 | tf_op jit(solution)/shard_map/mkc,mkr->cr/dot_general | solution.py:150
  132.1 5.1 %collective-permute-done.9 = f32[56,896]{1,0:T(8,128)S(1)} collective-permute-done((f32[56,896]{1,0:T(8,128)}, f32[56,896]{1,0:T(8,128)S(1)}, u32[]{:S(2)}, u32[]{:S(2)}) %collective-permute-start.9) | collective-permute-done | bytes 200736 | tf_op jit(solution)/shard_map/ppermute | solution.py:15
  140.4 3.0 %collective-permute-start.11 = (f32[112,896]{1,0:T(8,128)}, f32[112,896]{1,0:T(8,128)}, u32[]{:S(2)}, u32[]{:S(2)}) collective-permute-start(f32[112,896]{1,0:T(8,128)} %get-tuple-element.38), channel_id=1, source_target_pairs={{0,56},{8,0},{16,8},{24,16},{32,24},{40,32},{48,40},{56,48},{1,57}... | collective-permute-start | bytes 1204232 | tf_op jit(solution)/shard_map/ppermute | solution.py:15
  143.3 7.9 %collective-permute-done.11 = f32[112,896]{1,0:T(8,128)} collective-permute-done((f32[112,896]{1,0:T(8,128)}, f32[112,896]{1,0:T(8,128)}, u32[]{:S(2)}, u32[]{:S(2)}) %collective-permute-start.11) | collective-permute-done | bytes 401440 | tf_op jit(solution)/shard_map/ppermute | solution.py:15
  151.2 2.2 collective-permute-done.12
  153.4 2.1 bitcast_add_fusion.2
  157.6 7.2 %collective-permute-done.13 = f32[112,896]{1,0:T(8,128)} collective-permute-done((f32[112,896]{1,0:T(8,128)}, f32[112,896]{1,0:T(8,128)}, u32[]{:S(2)}, u32[]{:S(2)}) %collective-permute-start.13) | collective-permute-done | bytes 401440 | tf_op jit(solution)/shard_map/ppermute | solution.py:15
  166.4 2.1 bitcast_add_fusion.6
  170.5 6.6 %collective-permute-done.16 = f32[112,896]{1,0:T(8,128)S(1)} collective-permute-done((f32[112,896]{1,0:T(8,128)}, f32[112,896]{1,0:T(8,128)S(1)}, u32[]{:S(2)}, u32[]{:S(2)}) %collective-permute-start.16) | collective-permute-done | bytes 401440 | tf_op jit(solution)/shard_map/ppermute | solution.py:15
  180.6 5.6 %in_row_order.1 = bf16[8,448,896]{2,1,0:T(8,128)(2,1)} custom-call(bf16[4,456,896]{2,1,0:T(8,128)(2,1)} %pad_maximum_fusion.ours_ref, bf16[4,456,896]{2,1,0:T(8,128)(2,1)} %collective-permute-done.23.theirs_ref), custom_call_target="tpu_custom_call" | custom-call | tf_op jit(solution)/shard_map/in_row_order/pallas_call | solution.py:84
  188.0 4.3 %multiply_reduce_fusion.4 = (f32[112]{0:T(128)S(1)}, f32[112]{0:T(128)S(1)}, f32[112]{0:T(128)S(1)}, f32[112,896]{1,0:T(8,128)S(1)}) fusion(f32[112,896]{1,0:T(8,128)S(1)} %get-tuple-element.32, bf16[112,896]{1,0:T(8,128)(2,1)S(1)} %get-tuple-element.31, f32[896]{0:T(1024)S(1)} %fusion.53, bf16[3584,896]{1,0:T(8,128)(2,1)} %bitcast.105, ...), kind=kOutput, calls=%fused_computation.83 | convolution fusion | flops 723537536 | bytes 8033088 | tf_op jit(solution)/shard_map/dot_general | solution.py:166
  197.0 2.2 collective-permute-done.25
  203.3 3.5 %collective-permute-done.29 = bf16[112,896]{1,0:T(8,128)(2,1)S(1)} collective-permute-done((bf16[112,896]{1,0:T(8,128)(2,1)S(1)}, bf16[112,896]{1,0:T(8,128)(2,1)S(1)}, u32[]{:S(2)}, u32[]{:S(2)}) %collective-permute-start.29) | collective-permute-done | bytes 200736 | tf_op jit(solution)/shard_map/ppermute | solution.py:15
  215.9 2.2 collective-permute-done.31
  220.1 18.8 %all_to_all.10 = bf16[8,2,112,112]{2,3,1,0:T(8,128)(2,1)S(1)} all-to-all(bf16[8,2,112,112]{2,3,1,0:T(8,128)(2,1)S(1)} %maximum_bitcast_fusion), channel_id=1, replica_groups=mesh['y'=4,'z'=8,'x'=4,'core'=2] {'z'}, dimensions={0} | all-to-all | bytes 802816 | tf_op jit(solution)/shard_map/all_to_all | solution.py:189
  (104 shorter events, 57.4 us)
Async XLA Ops:
  5.2 56.8 %all-to-all-start = ((bf16[8,120,448]{1,2,0:T(8,128)(2,1)}), bf16[8,120,448]{1,2,0:T(8,128)(2,1)S(1)}, u32[]{:S(2)}, u32[]{:S(2)}) async-start(bf16[8,120,448]{1,2,0:T(8,128)(2,1)} %broadcast_in_dim.38), calls=%async_computation | async-start | bytes 1835008 | tf_op jit(solution)/shard_map/all_to_all | solution.py:127
  14.4 42.7 %collective-permute-start.7 = (bf16[2,112,896]{2,1,0:T(8,128)(2,1)S(1)}, bf16[2,112,896]{2,1,0:T(8,128)(2,1)S(1)}, u32[]{:S(2)}, u32[]{:S(2)}) collective-permute-start(bf16[2,112,896]{2,1,0:T(8,128)(2,1)S(1)} %collective-permute-done.4), channel_id=1, source_target_pairs={{0,6},{2,0},{4,2},{6,4},{1,7},{3,1},{5,3},{7,5},{8,14},{10,8},{12,... | collective-permute-start | bytes 1204232 | tf_op jit(solution)/shard_map/ppermute | solution.py:15
  41.1 16.0 %collective-permute-start.6 = (bf16[2,112,896]{2,1,0:T(8,128)(2,1)S(1)}, bf16[2,112,896]{2,1,0:T(8,128)(2,1)S(1)}, u32[]{:S(2)}, u32[]{:S(2)}) collective-permute-start(bf16[2,112,896]{2,1,0:T(8,128)(2,1)S(1)} %collective-permute-done.4), channel_id=1, source_target_pairs={{0,4},{2,6},{4,0},{6,2},{1,5},{3,7},{5,1},{7,3},{8,12},{10,14},{12... | collective-permute-start | bytes 1204232 | tf_op jit(solution)/shard_map/ppermute | solution.py:15
  41.1 19.5 %collective-permute-start.5 = (bf16[2,112,896]{2,1,0:T(8,128)(2,1)S(1)}, bf16[2,112,896]{2,1,0:T(8,128)(2,1)S(1)}, u32[]{:S(2)}, u32[]{:S(2)}) collective-permute-start(bf16[2,112,896]{2,1,0:T(8,128)(2,1)S(1)} %collective-permute-done.4), channel_id=1, source_target_pairs={{0,2},{2,4},{4,6},{6,0},{1,3},{3,5},{5,7},{7,1},{8,10},{10,12},{12... | collective-permute-start | bytes 1204232 | tf_op jit(solution)/shard_map/ppermute | solution.py:15
  62.0 46.7 %collective-permute-start.8 = (bf16[4,2,112,896]{3,2,1,0:T(8,128)(2,1)}, bf16[4,2,112,896]{3,2,1,0:T(8,128)(2,1)}, u32[]{:S(2)}, u32[]{:S(2)}) collective-permute-start(bf16[4,2,112,896]{3,2,1,0:T(8,128)(2,1)} %pad_maximum_fusion.1), channel_id=1, source_target_pairs={{0,1},{1,0},{2,3},{3,2},{4,5},{5,4},{6,7},{7,6},{8,9},{9,8},{10,11... | collective-permute-start | bytes 4816904 | tf_op jit(solution)/shard_map/ppermute | solution.py:15
  65.0 21.3 %collective-permute-start.22 = (bf16[456,896]{1,0:T(8,128)(2,1)}, bf16[456,896]{1,0:T(8,128)(2,1)S(1)}, u32[]{:S(2)}, u32[]{:S(2)}) collective-permute-start(bf16[456,896]{1,0:T(8,128)(2,1)} %maximum_maximum_fusion), channel_id=1, source_target_pairs={{0,6},{2,0},{4,2},{6,4},{1,7},{3,1},{5,3},{7,5},{8,14},{10,8},{12,... | collective-permute-start | bytes 2451464 | tf_op jit(solution)/shard_map/ppermute | solution.py:15
  65.9 22.9 %collective-permute-start.21 = (bf16[456,896]{1,0:T(8,128)(2,1)}, bf16[456,896]{1,0:T(8,128)(2,1)}, u32[]{:S(2)}, u32[]{:S(2)}) collective-permute-start(bf16[456,896]{1,0:T(8,128)(2,1)} %maximum_maximum_fusion), channel_id=1, source_target_pairs={{0,4},{2,6},{4,0},{6,2},{1,5},{3,7},{5,1},{7,3},{8,12},{10,14},{12... | collective-permute-start | bytes 2451464 | tf_op jit(solution)/shard_map/ppermute | solution.py:15
  66.2 39.4 %collective-permute-start.20 = (bf16[456,896]{1,0:T(8,128)(2,1)}, bf16[456,896]{1,0:T(8,128)(2,1)}, u32[]{:S(2)}, u32[]{:S(2)}) collective-permute-start(bf16[456,896]{1,0:T(8,128)(2,1)} %maximum_maximum_fusion), channel_id=1, source_target_pairs={{0,2},{2,4},{4,6},{6,0},{1,3},{3,5},{5,7},{7,1},{8,10},{10,12},{12... | collective-permute-start | bytes 2451464 | tf_op jit(solution)/shard_map/ppermute | solution.py:15
  67.1 45.8 %collective-permute-start.2 = (bf16[4,112,896]{2,1,0:T(8,128)(2,1)}, bf16[4,112,896]{2,1,0:T(8,128)(2,1)}, u32[]{:S(2)}, u32[]{:S(2)}) collective-permute-start(bf16[4,112,896]{2,1,0:T(8,128)(2,1)} %param.3), channel_id=1, source_target_pairs={{0,192},{64,0},{128,64},{192,128},{1,193},{65,1},{129,65},{193,129... | collective-permute-start | bytes 2408456 | tf_op jit(solution)/shard_map/ppermute | solution.py:15
  86.3 26.6 %collective-permute-start.1 = (bf16[4,112,896]{2,1,0:T(8,128)(2,1)}, bf16[4,112,896]{2,1,0:T(8,128)(2,1)S(1)}, u32[]{:S(2)}, u32[]{:S(2)}) collective-permute-start(bf16[4,112,896]{2,1,0:T(8,128)(2,1)} %param.3), channel_id=1, source_target_pairs={{0,128},{64,192},{128,0},{192,64},{1,129},{65,193},{129,1},{193,65... | collective-permute-start | bytes 2408456 | tf_op jit(solution)/shard_map/ppermute | solution.py:15
  88.9 35.5 %collective-permute-start = (bf16[4,112,896]{2,1,0:T(8,128)(2,1)}, bf16[4,112,896]{2,1,0:T(8,128)(2,1)S(1)}, u32[]{:S(2)}, u32[]{:S(2)}) collective-permute-start(bf16[4,112,896]{2,1,0:T(8,128)(2,1)} %param.3), channel_id=1, source_target_pairs={{0,64},{64,128},{128,192},{192,0},{1,65},{65,129},{129,193},{193,1... | collective-permute-start | bytes 2408456 | tf_op jit(solution)/shard_map/ppermute | solution.py:15
  108.6 71.9 %collective-permute-start.23 = (bf16[4,456,896]{2,1,0:T(8,128)(2,1)}, bf16[4,456,896]{2,1,0:T(8,128)(2,1)}, u32[]{:S(2)}, u32[]{:S(2)}) collective-permute-start(bf16[4,456,896]{2,1,0:T(8,128)(2,1)} %pad_maximum_fusion.ours_ref), channel_id=1, source_target_pairs={{0,1},{1,0},{2,3},{3,2},{4,5},{5,4},{6,7},{7,6},{8,9},{9,8},{10,11... | collective-permute-start | bytes 9805832 | tf_op jit(solution)/shard_map/ppermute | solution.py:15
  130.6 7.9 %collective-permute-start.10 = (f32[56,896]{1,0:T(8,128)}, f32[56,896]{1,0:T(8,128)}, u32[]{:S(2)}, u32[]{:S(2)}) collective-permute-start(f32[56,896]{1,0:T(8,128)} %get-tuple-element.39), channel_id=1, source_target_pairs={{0,8},{8,16},{16,24},{24,32},{32,40},{40,48},{48,56},{56,0},{1,9},... | collective-permute-start | bytes 602120 | tf_op jit(solution)/shard_map/ppermute | solution.py:15
  140.4 10.9 %collective-permute-start.11 = (f32[112,896]{1,0:T(8,128)}, f32[112,896]{1,0:T(8,128)}, u32[]{:S(2)}, u32[]{:S(2)}) collective-permute-start(f32[112,896]{1,0:T(8,128)} %get-tuple-element.38), channel_id=1, source_target_pairs={{0,56},{8,0},{16,8},{24,16},{32,24},{40,32},{48,40},{56,48},{1,57}... | collective-permute-start | bytes 1204232 | tf_op jit(solution)/shard_map/ppermute | solution.py:15
  143.3 10.1 %collective-permute-start.12 = (f32[112,896]{1,0:T(8,128)}, f32[112,896]{1,0:T(8,128)}, u32[]{:S(2)}, u32[]{:S(2)}) collective-permute-start(f32[112,896]{1,0:T(8,128)} %get-tuple-element.37), channel_id=1, source_target_pairs={{0,8},{8,16},{16,24},{24,32},{32,40},{40,48},{48,56},{56,0},{1,9},... | collective-permute-start | bytes 1204232 | tf_op jit(solution)/shard_map/ppermute | solution.py:15
  155.6 9.3 %collective-permute-start.13 = (f32[112,896]{1,0:T(8,128)}, f32[112,896]{1,0:T(8,128)}, u32[]{:S(2)}, u32[]{:S(2)}) collective-permute-start(f32[112,896]{1,0:T(8,128)} %get-tuple-element.36), channel_id=1, source_target_pairs={{0,56},{8,0},{16,8},{24,16},{32,24},{40,32},{48,40},{56,48},{1,57}... | collective-permute-start | bytes 1204232 | tf_op jit(solution)/shard_map/ppermute | solution.py:15
  157.2 9.2 %collective-permute-start.14 = (f32[112,896]{1,0:T(8,128)}, f32[112,896]{1,0:T(8,128)}, u32[]{:S(2)}, u32[]{:S(2)}) collective-permute-start(f32[112,896]{1,0:T(8,128)} %get-tuple-element.35), channel_id=1, source_target_pairs={{0,8},{8,16},{16,24},{24,32},{32,40},{40,48},{48,56},{56,0},{1,9},... | collective-permute-start | bytes 1204232 | tf_op jit(solution)/shard_map/ppermute | solution.py:15
  168.5 8.6 %collective-permute-start.16 = (f32[112,896]{1,0:T(8,128)}, f32[112,896]{1,0:T(8,128)S(1)}, u32[]{:S(2)}, u32[]{:S(2)}) collective-permute-start(f32[112,896]{1,0:T(8,128)} %get-tuple-element.34), channel_id=1, source_target_pairs={{0,8},{8,16},{16,24},{24,32},{32,40},{40,48},{48,56},{56,0},{1,9},... | collective-permute-start | bytes 1204232 | tf_op jit(solution)/shard_map/ppermute | solution.py:15
  168.8 8.4 %collective-permute-start.15 = (f32[112,896]{1,0:T(8,128)}, f32[112,896]{1,0:T(8,128)S(1)}, u32[]{:S(2)}, u32[]{:S(2)}) collective-permute-start(f32[112,896]{1,0:T(8,128)} %get-tuple-element.33), channel_id=1, source_target_pairs={{0,56},{8,0},{16,8},{24,16},{32,24},{40,32},{48,40},{56,48},{1,57}... | collective-permute-start | bytes 1204232 | tf_op jit(solution)/shard_map/ppermute | solution.py:15
  178.2 8.7 %collective-permute-start.19 = (bf16[112,896]{1,0:T(8,128)(2,1)S(1)}, bf16[112,896]{1,0:T(8,128)(2,1)S(1)}, u32[]{:S(2)}, u32[]{:S(2)}) collective-permute-start(bf16[112,896]{1,0:T(8,128)(2,1)S(1)} %get-tuple-element.31), channel_id=1, source_target_pairs={{0,192},{64,0},{128,64},{192,128},{1,193},{65,1},{129,65},{193,129... | collective-permute-start | bytes 602120 | tf_op jit(solution)/shard_map/ppermute | solution.py:15
  178.5 8.4 %collective-permute-start.18 = (bf16[112,896]{1,0:T(8,128)(2,1)S(1)}, bf16[112,896]{1,0:T(8,128)(2,1)S(1)}, u32[]{:S(2)}, u32[]{:S(2)}) collective-permute-start(bf16[112,896]{1,0:T(8,128)(2,1)S(1)} %get-tuple-element.31), channel_id=1, source_target_pairs={{0,128},{64,192},{128,0},{192,64},{1,129},{65,193},{129,1},{193,65... | collective-permute-start | bytes 602120 | tf_op jit(solution)/shard_map/ppermute | solution.py:15
  178.9 9.1 %collective-permute-start.17 = (bf16[112,896]{1,0:T(8,128)(2,1)S(1)}, bf16[112,896]{1,0:T(8,128)(2,1)S(1)}, u32[]{:S(2)}, u32[]{:S(2)}) collective-permute-start(bf16[112,896]{1,0:T(8,128)(2,1)S(1)} %get-tuple-element.31), channel_id=1, source_target_pairs={{0,64},{64,128},{128,192},{192,0},{1,65},{65,129},{129,193},{193,1... | collective-permute-start | bytes 602120 | tf_op jit(solution)/shard_map/ppermute | solution.py:15
  201.5 7.3 %collective-permute-start.28 = (bf16[112,896]{1,0:T(8,128)(2,1)S(1)}, bf16[112,896]{1,0:T(8,128)(2,1)S(1)}, u32[]{:S(2)}, u32[]{:S(2)}) collective-permute-start(bf16[112,896]{1,0:T(8,128)(2,1)S(1)} %fusion.49), channel_id=1, source_target_pairs={{0,128},{64,192},{128,0},{192,64},{1,129},{65,193},{129,1},{193,65... | collective-permute-start | bytes 602120 | tf_op jit(solution)/shard_map/ppermute | solution.py:15
  202.9 8.0 %collective-permute-start.27 = (bf16[112,896]{1,0:T(8,128)(2,1)S(1)}, bf16[112,896]{1,0:T(8,128)(2,1)S(1)}, u32[]{:S(2)}, u32[]{:S(2)}) collective-permute-start(bf16[112,896]{1,0:T(8,128)(2,1)S(1)} %fusion.49), channel_id=1, source_target_pairs={{0,64},{64,128},{128,192},{192,0},{1,65},{65,129},{129,193},{193,1... | collective-permute-start | bytes 602120 | tf_op jit(solution)/shard_map/ppermute | solution.py:15
  (13 other events, 107.5 us)

commit v4 on v3

--- a/solution.py
+++ b/solution.py
@@ -95,17 +95,12 @@
 def shards(grams, weights):
     y, z, x = (lax.axis_index(a) for a in ("y", "z", "x"))
     core = lax.axis_index("core")
-    models, slab, _ = grams.shape
+    slab, wide = grams.shape[1], 2 * grams.shape[2]
     ny, nz, nx = (lax.axis_size(a) for a in ("y", "z", "x"))
     cols = weights.shape[2]
-    half = models // 2
     turn = (x - y) % nx
 
     w_slots = all_shifts(weights, "y")
-
-    chip_gram = core_pair(grams, 2)
-    wide = chip_gram.shape[2]
-    mine = lax.dynamic_slice_in_dim(chip_gram, core * half, half, 0)
 
     total = jnp.sum(grams.astype(F32), axis=0)
     row_of = lax.broadcasted_iota(jnp.int32, (slab, wide), 0) + z * slab
@@ -118,15 +113,14 @@
     low = diag - high - middle
     tail = jnp.concatenate([jnp.stack([high, middle, low]), jnp.zeros((5, wide // 2), F32)])
     total = jnp.concatenate([total, tail], axis=0).astype(BF16)
-    mine, total = lax.optimization_barrier((mine, total))
 
     mine = lax.ppermute(
-        mine, ("y", "x"), [(a * nx + b, b * nx + a) for a in range(ny) for b in range(nx)]
+        grams, ("y", "x"), [(a * nx + b, b * nx + a) for a in range(ny) for b in range(nx)]
     )
     total = jnp.broadcast_to(total, (nz, *total.shape))
     total = lax.all_to_all(total, "z", 0, 0, tiled=True)
     mine = jnp.stack(all_shifts(mine, "x"))
-    gram_slots = core_pair(mine, 1)
+    gram_slots = core_pair(mine, 3)
     gram_slots = rolled(gram_slots, turn)
 
     tail = total[:, slab:].astype(F32).sum(axis=0)

time: 242 us -> 244 us (level)
    ppermute x32 -> x31, starting transfers between devices: 52.5 us -> 54.3 us  [shift(): return lax.ppermute(x, axis, [(i, (i + by) % size) for i in range(size)])]
    ppermute x32 -> x31, waiting for transfers between devices: 116 us -> 117 us  [shift(): return lax.ppermute(x, axis, [(i, (i + by) % size) for i in range(size)])]
  transfers between devices with their start and end apart: 34 -> 33, of which waited for: 24 -> 23; matrix products, arithmetic and copies ran while one was open for 11% -> 11% of each run, Pallas kernels for 2% -> 2%
where the time goes in v4:
time: 244 us; the launch traced here: 243 us
  waiting for transfers between devices  117 us (48%)
  starting transfers between devices  63.6 us (26%)
  blocking collectives  18.8 us (8%)
  other arithmetic  18.7 us (8%)
  matrix products  11.6 us (5%)
  local copies, waits for them, and re-layouts  6.77 us (3%)
  Pallas kernels  5.62 us (2%)
    ppermute x31, waiting for transfers between devices, shift(): return lax.ppermute(x, axis, [(i, (i + by) % size) for i in range(size)])  117 us
    ppermute x31, starting transfers between devices, shift(): return lax.ppermute(x, axis, [(i, (i + by) % size) for i in range(size)])  54.3 us
    all_to_all x1, blocking collectives, shards(): got = lax.all_to_all(sent, 'z', 0, 0, tiled=True)  18.8 us
    all_to_all x1, starting transfers between devices, shards(): total = lax.all_to_all(total, 'z', 0, 0, tiled=True)  8.57 us
    dot_general x2, matrix products, apply(): product = jnp.dot(everyone, total, preferred_element_type=F32)  5.66 us
    pallas_call x1, Pallas kernels, in_row_order(): pl.pallas_call(kernel, out_shape=jax.ShapeDtypeStruct((2 * blocks, deep,...  5.62 us
  transfers between devices with their start and end apart: 33, of which 23 were waited for; matrix products, arithmetic and copies ran while one was open for 11% of the time, Pallas kernels for 2%

profile of v4, /device:TPU:32, one launch (start us, length us, event | category | flops | bytes accessed | tf_op | source)
XLA Modules:
  0.0 243.5 jit_solution(13561944674792917435)
XLA Ops:
  3.2 8.6 %all-to-all-start = ((bf16[8,120,448]{1,2,0:T(8,128)(2,1)}), bf16[8,120,448]{1,2,0:T(8,128)(2,1)S(1)}, u32[]{:S(2)}, u32[]{:S(2)}) async-start(bf16[8,120,448]{1,2,0:T(8,128)(2,1)} %broadcast_in_dim.38), calls=%async_computation | async-start | bytes 1835008 | tf_op jit(solution)/shard_map/all_to_all | solution.py:121
  12.5 28.8 %collective-permute-start.6 = (bf16[4,112,448]{2,1,0:T(8,128)(2,1)S(1)}, bf16[4,112,448]{2,1,0:T(8,128)(2,1)S(1)}, u32[]{:S(2)}, u32[]{:S(2)}) collective-permute-start(bf16[4,112,448]{2,1,0:T(8,128)(2,1)S(1)} %collective-permute-done.3), channel_id=1, source_target_pairs={{0,6},{2,0},{4,2},{6,4},{1,7},{3,1},{5,3},{7,5},{8,14},{10,8},{12,... | collective-permute-start | bytes 1204232 | tf_op jit(solution)/shard_map/ppermute | solution.py:15
  42.1 17.6 %collective-permute-done.6 = bf16[4,112,448]{2,1,0:T(8,128)(2,1)S(1)} collective-permute-done((bf16[4,112,448]{2,1,0:T(8,128)(2,1)S(1)}, bf16[4,112,448]{2,1,0:T(8,128)(2,1)S(1)}, u32[]{:S(2)}, u32[]{:S(2)}) %collective-permute-start.6) | collective-permute-done | bytes 401440 | tf_op jit(solution)/shard_map/ppermute | solution.py:15
  59.7 3.4 %collective-permute-done.4 = bf16[4,112,448]{2,1,0:T(8,128)(2,1)S(1)} collective-permute-done((bf16[4,112,448]{2,1,0:T(8,128)(2,1)S(1)}, bf16[4,112,448]{2,1,0:T(8,128)(2,1)S(1)}, u32[]{:S(2)}, u32[]{:S(2)}) %collective-permute-start.4) | collective-permute-done | bytes 401440 | tf_op jit(solution)/shard_map/ppermute | solution.py:15
  71.7 17.4 %collective-permute-done.21 = bf16[456,896]{1,0:T(8,128)(2,1)S(1)} collective-permute-done((bf16[456,896]{1,0:T(8,128)(2,1)}, bf16[456,896]{1,0:T(8,128)(2,1)S(1)}, u32[]{:S(2)}, u32[]{:S(2)}) %collective-permute-start.21) | collective-permute-done | bytes 817184 | tf_op jit(solution)/shard_map/ppermute | solution.py:15
  89.0 2.5 %collective-permute-done.20 = bf16[456,896]{1,0:T(8,128)(2,1)} collective-permute-done((bf16[456,896]{1,0:T(8,128)(2,1)}, bf16[456,896]{1,0:T(8,128)(2,1)}, u32[]{:S(2)}, u32[]{:S(2)}) %collective-permute-start.20) | collective-permute-done | bytes 817184 | tf_op jit(solution)/shard_map/ppermute | solution.py:15
  91.6 16.7 %collective-permute-done.19 = bf16[456,896]{1,0:T(8,128)(2,1)} collective-permute-done((bf16[456,896]{1,0:T(8,128)(2,1)}, bf16[456,896]{1,0:T(8,128)(2,1)}, u32[]{:S(2)}, u32[]{:S(2)}) %collective-permute-start.19) | collective-permute-done | bytes 817184 | tf_op jit(solution)/shard_map/ppermute | solution.py:15
  108.3 3.1 %pad_maximum_fusion.ours_ref = bf16[4,456,896]{2,1,0:T(8,128)(2,1)} fusion(bf16[1,456,896]{2,1,0:T(8,128)(2,1)S(1)} %bitcast.121, bf16[1,456,896]{2,1,0:T(8,128)(2,1)} %bitcast.26, bf16[1,456,896]{2,1,0:T(8,128)(2,1)} %bitcast.25, bf16[1,456,896]{2,1,0:T(8,128)(2,1)S(1)} %fusion.69), kind=kLoop, calls=%fused_computation.8 | loop fusion | flops 4902912 | bytes 6537216 | tf_op jit(solution)/shard_map/stack | solution.py:134
  115.7 11.3 %collective-permute-done = bf16[4,112,896]{2,1,0:T(8,128)(2,1)S(1)} collective-permute-done((bf16[4,112,896]{2,1,0:T(8,128)(2,1)}, bf16[4,112,896]{2,1,0:T(8,128)(2,1)S(1)}, u32[]{:S(2)}, u32[]{:S(2)}) %collective-permute-start) | collective-permute-done | bytes 802848 | tf_op jit(solution)/shard_map/ppermute | solution.py:15
  127.0 4.8 %bitcast_add_fusion = f32[896,896]{1,0:T(8,128)S(1)} fusion(f32[896,896,1]{0,1,2:T(8,128)S(1)} %fusion.43, bf16[4,112,896]{2,1,0:T(8,128)(2,1)S(1)} %get-tuple-element.32, bf16[4,112,896]{2,1,0:T(8,128)(2,1)S(1)} %get-tuple-element.31, bf16[4,112,896]{2,1,0:T(8,128)(2,1)S(1)} %get-tuple-element.29, bf16[4,112,896]{2,1,0:T(8,128)(2,1)S(1)} %get-tuple-element.30, ...), kind=kOutput, calls=%fused_computation.24 | convolution fusion | flops 2889334784 | bytes 12845056 | tf_op jit(solution)/shard_map/mkc,mkr->cr/dot_general | solution.py:144
  134.8 5.1 %collective-permute-done.8 = f32[56,896]{1,0:T(8,128)S(1)} collective-permute-done((f32[56,896]{1,0:T(8,128)}, f32[56,896]{1,0:T(8,128)S(1)}, u32[]{:S(2)}, u32[]{:S(2)}) %collective-permute-start.8) | collective-permute-done | bytes 200736 | tf_op jit(solution)/shard_map/ppermute | solution.py:15
  143.1 3.0 %collective-permute-start.10 = (f32[112,896]{1,0:T(8,128)}, f32[112,896]{1,0:T(8,128)}, u32[]{:S(2)}, u32[]{:S(2)}) collective-permute-start(f32[112,896]{1,0:T(8,128)} %get-tuple-element.40), channel_id=1, source_target_pairs={{0,56},{8,0},{16,8},{24,16},{32,24},{40,32},{48,40},{56,48},{1,57}... | collective-permute-start | bytes 1204232 | tf_op jit(solution)/shard_map/ppermute | solution.py:15
  146.0 7.9 %collective-permute-done.10 = f32[112,896]{1,0:T(8,128)} collective-permute-done((f32[112,896]{1,0:T(8,128)}, f32[112,896]{1,0:T(8,128)}, u32[]{:S(2)}, u32[]{:S(2)}) %collective-permute-start.10) | collective-permute-done | bytes 401440 | tf_op jit(solution)/shard_map/ppermute | solution.py:15
  153.9 2.2 collective-permute-done.11
  156.1 2.1 bitcast_add_fusion.2
  160.3 7.2 %collective-permute-done.12 = f32[112,896]{1,0:T(8,128)} collective-permute-done((f32[112,896]{1,0:T(8,128)}, f32[112,896]{1,0:T(8,128)}, u32[]{:S(2)}, u32[]{:S(2)}) %collective-permute-start.12) | collective-permute-done | bytes 401440 | tf_op jit(solution)/shard_map/ppermute | solution.py:15
  169.1 2.1 bitcast_add_fusion.6
  173.2 6.6 %collective-permute-done.15 = f32[112,896]{1,0:T(8,128)S(1)} collective-permute-done((f32[112,896]{1,0:T(8,128)}, f32[112,896]{1,0:T(8,128)S(1)}, u32[]{:S(2)}, u32[]{:S(2)}) %collective-permute-start.15) | collective-permute-done | bytes 401440 | tf_op jit(solution)/shard_map/ppermute | solution.py:15
  183.1 5.6 %in_row_order.1 = bf16[8,448,896]{2,1,0:T(8,128)(2,1)} custom-call(bf16[4,456,896]{2,1,0:T(8,128)(2,1)} %pad_maximum_fusion.ours_ref, bf16[4,456,896]{2,1,0:T(8,128)(2,1)} %collective-permute-done.22.theirs_ref), custom_call_target="tpu_custom_call" | custom-call | tf_op jit(solution)/shard_map/in_row_order/pallas_call | solution.py:84
  190.5 4.3 %multiply_reduce_fusion.4 = (f32[112]{0:T(128)S(1)}, f32[112]{0:T(128)S(1)}, f32[112]{0:T(128)S(1)}, f32[112,896]{1,0:T(8,128)S(1)}) fusion(f32[112,896]{1,0:T(8,128)S(1)} %get-tuple-element.28, bf16[112,896]{1,0:T(8,128)(2,1)S(1)} %get-tuple-element.27, f32[896]{0:T(1024)S(1)} %fusion.52, bf16[3584,896]{1,0:T(8,128)(2,1)} %bitcast.105, ...), kind=kOutput, calls=%fused_computation.78 | convolution fusion | flops 723537536 | bytes 8033088 | tf_op jit(solution)/shard_map/dot_general | solution.py:160
  199.5 2.2 collective-permute-done.24
  205.7 3.5 %collective-permute-done.28 = bf16[112,896]{1,0:T(8,128)(2,1)S(1)} collective-permute-done((bf16[112,896]{1,0:T(8,128)(2,1)S(1)}, bf16[112,896]{1,0:T(8,128)(2,1)S(1)}, u32[]{:S(2)}, u32[]{:S(2)}) %collective-permute-start.28) | collective-permute-done | bytes 200736 | tf_op jit(solution)/shard_map/ppermute | solution.py:15
  218.4 2.2 collective-permute-done.30
  222.6 18.8 %all_to_all.10 = bf16[8,2,112,112]{2,3,1,0:T(8,128)(2,1)S(1)} all-to-all(bf16[8,2,112,112]{2,3,1,0:T(8,128)(2,1)S(1)} %maximum_bitcast_fusion), channel_id=1, replica_groups=mesh['y'=4,'z'=8,'x'=4,'core'=2] {'z'}, dimensions={0} | all-to-all | bytes 802816 | tf_op jit(solution)/shard_map/all_to_all | solution.py:183
  (106 shorter events, 55.3 us)
Async XLA Ops:
  3.2 61.5 %all-to-all-start = ((bf16[8,120,448]{1,2,0:T(8,128)(2,1)}), bf16[8,120,448]{1,2,0:T(8,128)(2,1)S(1)}, u32[]{:S(2)}, u32[]{:S(2)}) async-start(bf16[8,120,448]{1,2,0:T(8,128)(2,1)} %broadcast_in_dim.38), calls=%async_computation | async-start | bytes 1835008 | tf_op jit(solution)/shard_map/all_to_all | solution.py:121
  12.5 47.3 %collective-permute-start.6 = (bf16[4,112,448]{2,1,0:T(8,128)(2,1)S(1)}, bf16[4,112,448]{2,1,0:T(8,128)(2,1)S(1)}, u32[]{:S(2)}, u32[]{:S(2)}) collective-permute-start(bf16[4,112,448]{2,1,0:T(8,128)(2,1)S(1)} %collective-permute-done.3), channel_id=1, source_target_pairs={{0,6},{2,0},{4,2},{6,4},{1,7},{3,1},{5,3},{7,5},{8,14},{10,8},{12,... | collective-permute-start | bytes 1204232 | tf_op jit(solution)/shard_map/ppermute | solution.py:15
  41.3 18.5 %collective-permute-start.5 = (bf16[4,112,448]{2,1,0:T(8,128)(2,1)S(1)}, bf16[4,112,448]{2,1,0:T(8,128)(2,1)S(1)}, u32[]{:S(2)}, u32[]{:S(2)}) collective-permute-start(bf16[4,112,448]{2,1,0:T(8,128)(2,1)S(1)} %collective-permute-done.3), channel_id=1, source_target_pairs={{0,4},{2,6},{4,0},{6,2},{1,5},{3,7},{5,1},{7,3},{8,12},{10,14},{12... | collective-permute-start | bytes 1204232 | tf_op jit(solution)/shard_map/ppermute | solution.py:15
  41.3 21.9 %collective-permute-start.4 = (bf16[4,112,448]{2,1,0:T(8,128)(2,1)S(1)}, bf16[4,112,448]{2,1,0:T(8,128)(2,1)S(1)}, u32[]{:S(2)}, u32[]{:S(2)}) collective-permute-start(bf16[4,112,448]{2,1,0:T(8,128)(2,1)S(1)} %collective-permute-done.3), channel_id=1, source_target_pairs={{0,2},{2,4},{4,6},{6,0},{1,3},{3,5},{5,7},{7,1},{8,10},{10,12},{12... | collective-permute-start | bytes 1204232 | tf_op jit(solution)/shard_map/ppermute | solution.py:15
  64.7 46.8 %collective-permute-start.7 = (bf16[4,4,112,448]{3,2,1,0:T(8,128)(2,1)}, bf16[4,4,112,448]{3,2,1,0:T(8,128)(2,1)}, u32[]{:S(2)}, u32[]{:S(2)}) collective-permute-start(bf16[4,4,112,448]{3,2,1,0:T(8,128)(2,1)} %pad_maximum_fusion.1), channel_id=1, source_target_pairs={{0,1},{1,0},{2,3},{3,2},{4,5},{5,4},{6,7},{7,6},{8,9},{9,8},{10,11... | collective-permute-start | bytes 4816904 | tf_op jit(solution)/shard_map/ppermute | solution.py:15
  67.7 21.3 %collective-permute-start.21 = (bf16[456,896]{1,0:T(8,128)(2,1)}, bf16[456,896]{1,0:T(8,128)(2,1)S(1)}, u32[]{:S(2)}, u32[]{:S(2)}) collective-permute-start(bf16[456,896]{1,0:T(8,128)(2,1)} %maximum_maximum_fusion), channel_id=1, source_target_pairs={{0,6},{2,0},{4,2},{6,4},{1,7},{3,1},{5,3},{7,5},{8,14},{10,8},{12,... | collective-permute-start | bytes 2451464 | tf_op jit(solution)/shard_map/ppermute | solution.py:15
  68.6 22.9 %collective-permute-start.20 = (bf16[456,896]{1,0:T(8,128)(2,1)}, bf16[456,896]{1,0:T(8,128)(2,1)}, u32[]{:S(2)}, u32[]{:S(2)}) collective-permute-start(bf16[456,896]{1,0:T(8,128)(2,1)} %maximum_maximum_fusion), channel_id=1, source_target_pairs={{0,4},{2,6},{4,0},{6,2},{1,5},{3,7},{5,1},{7,3},{8,12},{10,14},{12... | collective-permute-start | bytes 2451464 | tf_op jit(solution)/shard_map/ppermute | solution.py:15
  68.9 39.4 %collective-permute-start.19 = (bf16[456,896]{1,0:T(8,128)(2,1)}, bf16[456,896]{1,0:T(8,128)(2,1)}, u32[]{:S(2)}, u32[]{:S(2)}) collective-permute-start(bf16[456,896]{1,0:T(8,128)(2,1)} %maximum_maximum_fusion), channel_id=1, source_target_pairs={{0,2},{2,4},{4,6},{6,0},{1,3},{3,5},{5,7},{7,1},{8,10},{10,12},{12... | collective-permute-start | bytes 2451464 | tf_op jit(solution)/shard_map/ppermute | solution.py:15
  69.8 45.9 %collective-permute-start.2 = (bf16[4,112,896]{2,1,0:T(8,128)(2,1)}, bf16[4,112,896]{2,1,0:T(8,128)(2,1)}, u32[]{:S(2)}, u32[]{:S(2)}) collective-permute-start(bf16[4,112,896]{2,1,0:T(8,128)(2,1)} %param.3), channel_id=1, source_target_pairs={{0,192},{64,0},{128,64},{192,128},{1,193},{65,1},{129,65},{193,129... | collective-permute-start | bytes 2408456 | tf_op jit(solution)/shard_map/ppermute | solution.py:15
  89.0 26.7 %collective-permute-start.1 = (bf16[4,112,896]{2,1,0:T(8,128)(2,1)}, bf16[4,112,896]{2,1,0:T(8,128)(2,1)S(1)}, u32[]{:S(2)}, u32[]{:S(2)}) collective-permute-start(bf16[4,112,896]{2,1,0:T(8,128)(2,1)} %param.3), channel_id=1, source_target_pairs={{0,128},{64,192},{128,0},{192,64},{1,129},{65,193},{129,1},{193,65... | collective-permute-start | bytes 2408456 | tf_op jit(solution)/shard_map/ppermute | solution.py:15
  91.6 35.5 %collective-permute-start = (bf16[4,112,896]{2,1,0:T(8,128)(2,1)}, bf16[4,112,896]{2,1,0:T(8,128)(2,1)S(1)}, u32[]{:S(2)}, u32[]{:S(2)}) collective-permute-start(bf16[4,112,896]{2,1,0:T(8,128)(2,1)} %param.3), channel_id=1, source_target_pairs={{0,64},{64,128},{128,192},{192,0},{1,65},{65,129},{129,193},{193,1... | collective-permute-start | bytes 2408456 | tf_op jit(solution)/shard_map/ppermute | solution.py:15
  111.4 71.7 %collective-permute-start.22 = (bf16[4,456,896]{2,1,0:T(8,128)(2,1)}, bf16[4,456,896]{2,1,0:T(8,128)(2,1)}, u32[]{:S(2)}, u32[]{:S(2)}) collective-permute-start(bf16[4,456,896]{2,1,0:T(8,128)(2,1)} %pad_maximum_fusion.ours_ref), channel_id=1, source_target_pairs={{0,1},{1,0},{2,3},{3,2},{4,5},{5,4},{6,7},{7,6},{8,9},{9,8},{10,11... | collective-permute-start | bytes 9805832 | tf_op jit(solution)/shard_map/ppermute | solution.py:15
  133.1 8.1 %collective-permute-start.9 = (f32[56,896]{1,0:T(8,128)}, f32[56,896]{1,0:T(8,128)}, u32[]{:S(2)}, u32[]{:S(2)}) collective-permute-start(f32[56,896]{1,0:T(8,128)} %get-tuple-element.41), channel_id=1, source_target_pairs={{0,8},{8,16},{16,24},{24,32},{32,40},{40,48},{48,56},{56,0},{1,9},... | collective-permute-start | bytes 602120 | tf_op jit(solution)/shard_map/ppermute | solution.py:15
  143.1 10.9 %collective-permute-start.10 = (f32[112,896]{1,0:T(8,128)}, f32[112,896]{1,0:T(8,128)}, u32[]{:S(2)}, u32[]{:S(2)}) collective-permute-start(f32[112,896]{1,0:T(8,128)} %get-tuple-element.40), channel_id=1, source_target_pairs={{0,56},{8,0},{16,8},{24,16},{32,24},{40,32},{48,40},{56,48},{1,57}... | collective-permute-start | bytes 1204232 | tf_op jit(solution)/shard_map/ppermute | solution.py:15
  146.0 10.1 %collective-permute-start.11 = (f32[112,896]{1,0:T(8,128)}, f32[112,896]{1,0:T(8,128)}, u32[]{:S(2)}, u32[]{:S(2)}) collective-permute-start(f32[112,896]{1,0:T(8,128)} %get-tuple-element.39), channel_id=1, source_target_pairs={{0,8},{8,16},{16,24},{24,32},{32,40},{40,48},{48,56},{56,0},{1,9},... | collective-permute-start | bytes 1204232 | tf_op jit(solution)/shard_map/ppermute | solution.py:15
  158.3 9.3 %collective-permute-start.12 = (f32[112,896]{1,0:T(8,128)}, f32[112,896]{1,0:T(8,128)}, u32[]{:S(2)}, u32[]{:S(2)}) collective-permute-start(f32[112,896]{1,0:T(8,128)} %get-tuple-element.38), channel_id=1, source_target_pairs={{0,56},{8,0},{16,8},{24,16},{32,24},{40,32},{48,40},{56,48},{1,57}... | collective-permute-start | bytes 1204232 | tf_op jit(solution)/shard_map/ppermute | solution.py:15
  159.9 9.2 %collective-permute-start.13 = (f32[112,896]{1,0:T(8,128)}, f32[112,896]{1,0:T(8,128)}, u32[]{:S(2)}, u32[]{:S(2)}) collective-permute-start(f32[112,896]{1,0:T(8,128)} %get-tuple-element.37), channel_id=1, source_target_pairs={{0,8},{8,16},{16,24},{24,32},{32,40},{40,48},{48,56},{56,0},{1,9},... | collective-permute-start | bytes 1204232 | tf_op jit(solution)/shard_map/ppermute | solution.py:15
  171.2 8.6 %collective-permute-start.15 = (f32[112,896]{1,0:T(8,128)}, f32[112,896]{1,0:T(8,128)S(1)}, u32[]{:S(2)}, u32[]{:S(2)}) collective-permute-start(f32[112,896]{1,0:T(8,128)} %get-tuple-element.36), channel_id=1, source_target_pairs={{0,8},{8,16},{16,24},{24,32},{32,40},{40,48},{48,56},{56,0},{1,9},... | collective-permute-start | bytes 1204232 | tf_op jit(solution)/shard_map/ppermute | solution.py:15
  171.5 8.4 %collective-permute-start.14 = (f32[112,896]{1,0:T(8,128)}, f32[112,896]{1,0:T(8,128)S(1)}, u32[]{:S(2)}, u32[]{:S(2)}) collective-permute-start(f32[112,896]{1,0:T(8,128)} %get-tuple-element.35), channel_id=1, source_target_pairs={{0,56},{8,0},{16,8},{24,16},{32,24},{40,32},{48,40},{56,48},{1,57}... | collective-permute-start | bytes 1204232 | tf_op jit(solution)/shard_map/ppermute | solution.py:15
  180.9 8.5 %collective-permute-start.18 = (bf16[112,896]{1,0:T(8,128)(2,1)S(1)}, bf16[112,896]{1,0:T(8,128)(2,1)S(1)}, u32[]{:S(2)}, u32[]{:S(2)}) collective-permute-start(bf16[112,896]{1,0:T(8,128)(2,1)S(1)} %get-tuple-element.27), channel_id=1, source_target_pairs={{0,192},{64,0},{128,64},{192,128},{1,193},{65,1},{129,65},{193,129... | collective-permute-start | bytes 602120 | tf_op jit(solution)/shard_map/ppermute | solution.py:15
  181.0 8.4 %collective-permute-start.17 = (bf16[112,896]{1,0:T(8,128)(2,1)S(1)}, bf16[112,896]{1,0:T(8,128)(2,1)S(1)}, u32[]{:S(2)}, u32[]{:S(2)}) collective-permute-start(bf16[112,896]{1,0:T(8,128)(2,1)S(1)} %get-tuple-element.27), channel_id=1, source_target_pairs={{0,128},{64,192},{128,0},{192,64},{1,129},{65,193},{129,1},{193,65... | collective-permute-start | bytes 602120 | tf_op jit(solution)/shard_map/ppermute | solution.py:15
  181.4 9.1 %collective-permute-start.16 = (bf16[112,896]{1,0:T(8,128)(2,1)S(1)}, bf16[112,896]{1,0:T(8,128)(2,1)S(1)}, u32[]{:S(2)}, u32[]{:S(2)}) collective-permute-start(bf16[112,896]{1,0:T(8,128)(2,1)S(1)} %get-tuple-element.27), channel_id=1, source_target_pairs={{0,64},{64,128},{128,192},{192,0},{1,65},{65,129},{129,193},{193,1... | collective-permute-start | bytes 602120 | tf_op jit(solution)/shard_map/ppermute | solution.py:15
  204.0 7.3 %collective-permute-start.27 = (bf16[112,896]{1,0:T(8,128)(2,1)S(1)}, bf16[112,896]{1,0:T(8,128)(2,1)S(1)}, u32[]{:S(2)}, u32[]{:S(2)}) collective-permute-start(bf16[112,896]{1,0:T(8,128)(2,1)S(1)} %fusion.48), channel_id=1, source_target_pairs={{0,128},{64,192},{128,0},{192,64},{1,129},{65,193},{129,1},{193,65... | collective-permute-start | bytes 602120 | tf_op jit(solution)/shard_map/ppermute | solution.py:15
  205.4 8.0 %collective-permute-start.26 = (bf16[112,896]{1,0:T(8,128)(2,1)S(1)}, bf16[112,896]{1,0:T(8,128)(2,1)S(1)}, u32[]{:S(2)}, u32[]{:S(2)}) collective-permute-start(bf16[112,896]{1,0:T(8,128)(2,1)S(1)} %fusion.48), channel_id=1, source_target_pairs={{0,64},{64,128},{128,192},{192,0},{1,65},{65,129},{129,193},{193,1... | collective-permute-start | bytes 602120 | tf_op jit(solution)/shard_map/ppermute | solution.py:15
  (15 other events, 118.0 us)
